TPU v7x, 256 devices: a whole 4x4x8 slice. The times are simulated.
256 devices in a mesh: src: 16 (over x_hi, z), tgt: 16 (over x_lo, y, core).
Axes of the slice: x: 4 (x_hi: 2, x_lo: 2; x = x_hi * 2 + x_lo), y: 4, z: 8, core: 2. Of those that a mesh axis runs over, the one named last changes fastest.
Arguments:
- source_words: bfloat16 [32768, 300], P(('src', 'tgt')), may hold values from -3 to 3
- target_words: bfloat16 [30720, 300], P(('tgt', 'src')), may hold values from -24 to 24
Outputs:
- rotated: bfloat16 [32768, 300], P(('src', 'tgt'))
- matched: float32 [32768, 300], P(('src', 'tgt'))
- ortho: float32 [300, 300], replicated
- row_pot: float32 [32768], P(('src', 'tgt'))
- col_pot: float32 [30720], P(('tgt', 'src'))
All inputs are finite; a program needn't handle non-finite values.
Results may differ from a plain program's by a relative error of at most 0.0034.
Values may be sent and summed in bfloat16 or wider, within the bound.
A program may use at most 64 MiB of HBM per device.

v0:
```python
import math

import jax
import jax.numpy as jnp
from jax import lax
from jax.sharding import PartitionSpec as P

ITERS = 2
NEWTON = 12


def sent_to_all(array, axis):
    copies = jnp.broadcast_to(array, (lax.axis_size(axis), *array.shape))
    return lax.all_to_all(copies, axis, split_axis=0, concat_axis=0, tiled=True)


def collected_together(array, axis):
    leaves = jax.tree.leaves(array)
    sequence = sorted(range(len(leaves)), key=lambda k: -leaves[k].size)
    width = (1, *leaves[sequence[0]].shape)[-1]
    lines = [
        jnp.pad(leaves[k].reshape(-1), (0, -leaves[k].size % width)).reshape(-1, width)
        for k in sequence
    ]
    both, at, found = (sent_to_all(jnp.concatenate(lines), axis), 0, {})
    for k, line in zip(sequence, lines):
        share = both[:, at : at + len(line)].reshape(len(both), -1)
        found[k] = share[:, : leaves[k].size].reshape(-1, *leaves[k].shape)
        at += len(line)
    numbers = iter(range(len(leaves)))
    return jax.tree.map(lambda _: found[next(numbers)], array)


def folded_in_pairs(pieces, combine):
    while len(jax.tree.leaves(pieces)[0]) > 1:
        pieces = jax.vmap(combine)(
            *(jax.tree.map(lambda part: part[side::2], pieces) for side in (0, 1))
        )
    return jax.tree.map(lambda part: part[0], pieces)


def combined_all(array, axis, combine):
    pieces = collected_together(array, axis)
    return folded_in_pairs(pieces, combine)


def gathered_by_type(array, axis):
    leaves, found = (jax.tree.leaves(array), {})
    for first, a in enumerate(leaves):
        if first not in found:
            alike = [k for k, b in enumerate(leaves) if b.dtype == a.dtype]
            got = (
                collected_together([leaves[k] for k in alike], axis)
                if len(alike) > 1
                else [sent_to_all(a, axis)]
            )
            for k, b in zip(alike, got):
                found[k] = b
    numbers = iter(range(len(leaves)))
    return jax.tree.map(lambda _: found[next(numbers)], array)


def combined_all_2(array, axis, combine):
    pieces = gathered_by_type(array, axis)
    return folded_in_pairs(pieces, combine)


def joined_along(blocks, dim):
    lengths = list(blocks.shape[1:])
    lengths[dim] *= blocks.shape[0]
    return jnp.moveaxis(blocks, 0, dim).reshape(lengths)


def collect(array, axis, dim):
    return joined_along(sent_to_all(array, axis), dim)


def split_up(array, dim, size):
    lengths = array.shape
    blocks = array.reshape(*lengths[:dim], size, lengths[dim] // size, *lengths[dim + 1 :])
    return jnp.moveaxis(blocks, dim, 0)


def summed_on_arrival(array, axis, dim):
    blocks = split_up(array, dim, lax.axis_size(axis))
    arrived = lax.all_to_all(blocks, axis, split_axis=0, concat_axis=0, tiled=True)
    return arrived.sum(axis=0)


def combine(first, second):
    higher = jnp.maximum(first[0], second[0])
    return (higher, first[1] * jnp.exp(first[0] - higher) + second[1] * jnp.exp(second[0] - higher))


def reduce_rows(top, total):
    higher, whole = combined_all((top, total), "tgt", combine)
    return -(higher + jnp.log(whole))


def reduce_cols(top, total):
    higher, whole = combined_all_2((top, total), "src", combine)
    return -(higher + jnp.log(whole))


def body(source_words, target_words):
    width = source_words.shape[1]
    scale = 4.0 / math.sqrt(width)
    highest = lax.Precision.HIGHEST
    src_block = collect(source_words, "tgt", 0)
    rows = src_block.shape[0]
    cols = target_words.shape[0] * lax.axis_size("src")
    inner = (((1,), (1,)), ((), ()))
    leading = (((0,), (0,)), ((), ()))

    def scores(piece):
        return lax.dot_general(src_block, piece, inner, preferred_element_type=jnp.float32) * scale

    col_pot = jnp.zeros((cols,), jnp.float32)
    row_pot = jnp.zeros((rows,), jnp.float32)
    for sweep_index in range(ITERS):
        row_top = jnp.full((rows,), -jnp.inf, jnp.float32)
        total = jnp.zeros((rows,), jnp.float32)
        row_shift = col_pot
        row_logits = scores(collect(target_words, "src", 0)) + row_shift[None, :]
        higher = jnp.maximum(row_top, jnp.max(row_logits, axis=1))
        total = total * jnp.exp(row_top - higher) + jnp.sum(
            jnp.exp(row_logits - higher[:, None]), axis=1
        )
        top, total = (higher, total)
        row_pot = reduce_rows(top, total)
        logits = scores(collect(target_words, "src", 0)) + row_pot[:, None]
        col_top = jnp.max(logits, axis=0)
        parts = jnp.stack([col_top, jnp.sum(jnp.exp(logits - col_top[None, :]), axis=0)])
        col_pot = reduce_cols(parts[0], parts[1])
    piece = collect(target_words, "src", 0)
    plan = jnp.exp(scores(piece) + row_pot[:, None] + col_pot[None, :]).astype(jnp.bfloat16)
    summed = jnp.dot(plan, piece, preferred_element_type=jnp.float32)
    matched = summed_on_arrival(summed, "tgt", 0)
    term = lax.dot_general(src_block.astype(jnp.float32), summed, leading, precision=highest)
    cov = lax.psum(term, ("src", "tgt"))
    ortho = cov / jnp.sqrt(jnp.sum(cov * cov) + 1e-06)
    for step_index in range(NEWTON):
        ortho = 1.5 * ortho - 0.5 * jnp.dot(
            ortho, jnp.dot(ortho.T, ortho, precision=highest), precision=highest
        )
    rotated = jnp.dot(source_words.astype(jnp.float32), ortho, precision=highest).astype(
        jnp.bfloat16
    )
    own_rows = rows // lax.axis_size("tgt")
    own_cols = cols // lax.axis_size("src")
    row_part = lax.dynamic_slice_in_dim(row_pot, lax.axis_index("tgt") * own_rows, own_rows)
    col_part = lax.dynamic_slice_in_dim(col_pot, lax.axis_index("src") * own_cols, own_cols)
    return (rotated, matched, ortho, row_part, col_part)


def solution(mesh):
    in_specs = (P(("src", "tgt"), None), P(("tgt", "src"), None))
    out_specs = (
        P(("src", "tgt"), None),
        P(("src", "tgt"), None),
        P(),
        P(("src", "tgt")),
        P(("tgt", "src")),
    )
    return jax.shard_map(body, mesh=mesh, in_specs=in_specs, out_specs=out_specs, check_vma=False)
```

profile of v0, /device:TPU:1, one launch (start us, length us, event | category | flops | bytes accessed | tf_op | source)
XLA Modules:
  0.0 514.6 jit_solution(17925122348003594462)
XLA Ops:
  8.2 24.6 %all_to_all.39 = bf16[16,128,300]{1,2,0:T(8,128)(2,1)S(1)} all-to-all(bf16[16,128,300]{1,2,0:T(8,128)(2,1)S(1)} %broadcast_in_dim.12), channel_id=1, replica_groups=mesh['src'=16,'tgt'=16] {'tgt'}, dimensions={0} | all-to-all | bytes 2457600 | tf_op jit(solution)/shard_map/all_to_all | solution.py:14
  34.9 10.5 %all-to-all-start.1 = ((bf16[16,120,300]{1,2,0:T(8,128)(2,1)}), bf16[16,120,300]{1,2,0:T(8,128)(2,1)S(1)}, u32[]{:S(2)}, u32[]{:S(2)}) async-start(bf16[16,120,300]{1,2,0:T(8,128)(2,1)} %broadcast_in_dim.13), calls=%async_computation.1 | async-start | bytes 2490368 | tf_op jit(solution)/shard_map/all_to_all | solution.py:14
  46.2 30.0 %all-to-all-done.1 = bf16[16,120,300]{1,2,0:T(8,128)(2,1)S(1)} async-done(((bf16[16,120,300]{1,2,0:T(8,128)(2,1)}), bf16[16,120,300]{1,2,0:T(8,128)(2,1)S(1)}, u32[]{:S(2)}, u32[]{:S(2)}) %all-to-all-start.1) | async-done | bytes 1152032 | tf_op jit(solution)/shard_map/all_to_all | solution.py:14
  77.6 2.7 reshape.145
  80.3 7.9 %fusion.30 = (f32[2048]{0:T(1024)S(1)}, f32[2048,1920]{1,0:T(8,128)}) fusion(bf16[2048,300]{0,1:T(8,128)(2,1)S(1)} %bitcast.103, bf16[1920,300]{0,1:T(8,128)(2,1)S(1)} %reshape.145), kind=kOutput, calls=%fused_computation.101 | convolution fusion | flops 2367158272 | bytes 18117632 | tf_op jit(solution)/shard_map/dot_general | solution.py:116
  88.3 7.7 %exponential_reduce_fusion.3 = f32[2048]{0:T(1024)S(1)} fusion(f32[2048,1920]{1,0:T(8,128)} %get-tuple-element.55, f32[2048]{0:T(1024)S(1)} %get-tuple-element.54), kind=kLoop, calls=%fused_computation.4 | loop fusion | flops 7862272 | bytes 15745024 | tf_op jit(solution)/shard_map/reduce_sum | solution.py:126
  96.1 12.9 %all_to_all.40 = f32[16,2,2048]{2,1,0:T(2,128)S(1)} all-to-all(f32[16,2,2048]{2,1,0:T(2,128)S(1)} %broadcast_in_dim.14), channel_id=1, replica_groups=mesh['src'=16,'tgt'=16] {'tgt'}, dimensions={0} | all-to-all | bytes 524288 | tf_op jit(solution)/shard_map/all_to_all | solution.py:14
  109.8 6.6 %add_reduce_fusion.1 = f32[1920]{0:T(1024)S(1)} fusion(f32[2048,1920]{1,0:T(8,128)} %get-tuple-element.55, f32[2048]{0:T(1024)S(1)} %bitcast.127), kind=kLoop, calls=%fused_computation.6 | loop fusion | flops 7862400 | bytes 15744512 | tf_op jit(solution)/shard_map/reduce_max | solution.py:132
  116.4 8.1 %exponential_reduce_fusion.2 = f32[1920]{0:T(1024)S(1)} fusion(f32[2048,1920]{1,0:T(8,128)} %get-tuple-element.55, f32[1920]{0:T(1024)S(1)} %add_reduce_fusion.1, f32[2048]{0:T(1024)S(1)} %bitcast.128), kind=kLoop, calls=%fused_computation.3 | loop fusion | flops 11794560 | bytes 15752192 | tf_op jit(solution)/shard_map/reduce_sum | solution.py:133
  124.6 13.4 %all_to_all.41 = f32[16,2,1920]{2,1,0:T(2,128)S(1)} all-to-all(f32[16,2,1920]{2,1,0:T(2,128)S(1)} %broadcast_in_dim.15), channel_id=1, replica_groups=mesh['src'=16,'tgt'=16] {'src'}, dimensions={0} | all-to-all | bytes 491520 | tf_op jit(solution)/shard_map/all_to_all | solution.py:14
  138.8 6.6 %add_reduce_fusion = f32[2048]{0:T(1024)S(1)} fusion(f32[2048,1920]{1,0:T(8,128)} %get-tuple-element.55, f32[1920]{0:T(1024)S(1)} %negate_reduce_fusion), kind=kLoop, calls=%fused_computation.5 | loop fusion | flops 7862272 | bytes 15744512 | tf_op jit(solution)/shard_map/reduce_max | solution.py:125
  145.4 8.2 %exponential_reduce_fusion.1 = f32[2048]{0:T(1024)S(1)} fusion(f32[2048,1920]{1,0:T(8,128)} %get-tuple-element.55, f32[2048]{0:T(1024)S(1)} %add_reduce_fusion, f32[1920]{0:T(1024)S(1)} %negate_reduce_fusion), kind=kLoop, calls=%fused_computation.2 | loop fusion | flops 11794432 | bytes 15752704 | tf_op jit(solution)/shard_map/reduce_sum | solution.py:126
  153.7 13.4 %all_to_all.42 = f32[16,2,2048]{2,1,0:T(2,128)S(1)} all-to-all(f32[16,2,2048]{2,1,0:T(2,128)S(1)} %broadcast_in_dim.16), channel_id=1, replica_groups=mesh['src'=16,'tgt'=16] {'tgt'}, dimensions={0} | all-to-all | bytes 524288 | tf_op jit(solution)/shard_map/all_to_all | solution.py:14
  167.9 6.6 %add_reduce_fusion.2 = f32[1920]{0:T(1024)S(1)} fusion(f32[2048,1920]{1,0:T(8,128)} %get-tuple-element.55, f32[2048]{0:T(1024)S(1)} %bitcast.124), kind=kLoop, calls=%fused_computation.7 | loop fusion | flops 7862400 | bytes 15744512 | tf_op jit(solution)/shard_map/reduce_max | solution.py:132
  174.5 8.1 %exponential_reduce_fusion = f32[1920]{0:T(1024)S(1)} fusion(f32[2048,1920]{1,0:T(8,128)} %get-tuple-element.55, f32[1920]{0:T(1024)S(1)} %add_reduce_fusion.2, f32[2048]{0:T(1024)S(1)} %bitcast.125), kind=kLoop, calls=%fused_computation.1 | loop fusion | flops 11794560 | bytes 15752192 | tf_op jit(solution)/shard_map/reduce_sum | solution.py:133
  183.4 4.2 all-to-all-start.5
  188.2 8.7 %all-to-all-done.5 = f32[16,2,1920]{2,1,0:T(2,128)S(1)} async-done(((f32[16,2,1920]{2,1,0:T(2,128)}), f32[16,2,1920]{2,1,0:T(2,128)S(1)}, u32[]{:S(2)}, u32[]{:S(2)}) %all-to-all-start.5) | async-done | bytes 245792 | tf_op jit(solution)/shard_map/all_to_all | solution.py:14
  197.7 9.8 %fusion = f32[2048,300]{0,1:T(8,128)} fusion(bf16[1920,300]{0,1:T(8,128)(2,1)S(1)} %reshape.145, f32[2048,1920]{1,0:T(8,128)} %get-tuple-element.55, f32[1920]{0:T(1024)S(1)} %get-tuple-element.20, f32[2048]{0:T(1024)S(1)} %bitcast.126), kind=kOutput, calls=%fused_computation.9 | convolution fusion | flops 2371092480 | bytes 19354112 | tf_op jit(solution)/shard_map/dot_general | solution.py:137
  207.5 4.6 convolution_bitcast_fusion
  214.4 2.2 copy.60
  216.6 6.6 %all-to-all-start.6 = ((f32[16,128,300]{1,2,0:T(8,128)}), f32[16,128,300]{1,2,0:T(8,128)S(1)}, u32[]{:S(2)}, u32[]{:S(2)}) async-start(f32[16,128,300]{1,2,0:T(8,128)} %copy.60), calls=%async_computation.6 | async-start | bytes 4980736 | tf_op jit(solution)/shard_map/all_to_all | solution.py:86
  223.8 247.8 %all-reduce.2.cloned.1.call-done = f32[300,300]{0,1:T(8,128)} async-done(((f32[300,300]{0,1:T(8,128)}), f32[300,300]{0,1:T(8,128)}) %all-reduce.2.cloned.1.call-update) | async-done | bytes 360016 | tf_op jit(solution)/shard_map/psum | solution.py:140
  474.1 2.2 fusion.16
  476.3 2.4 fusion.14
  (130 shorter events, 43.1 us)
Async XLA Ops:
  34.9 41.4 %all-to-all-start.1 = ((bf16[16,120,300]{1,2,0:T(8,128)(2,1)}), bf16[16,120,300]{1,2,0:T(8,128)(2,1)S(1)}, u32[]{:S(2)}, u32[]{:S(2)}) async-start(bf16[16,120,300]{1,2,0:T(8,128)(2,1)} %broadcast_in_dim.13), calls=%async_computation.1 | async-start | bytes 2490368 | tf_op jit(solution)/shard_map/all_to_all | solution.py:14
  183.4 13.5 %all-to-all-start.5 = ((f32[16,2,1920]{2,1,0:T(2,128)}), f32[16,2,1920]{2,1,0:T(2,128)S(1)}, u32[]{:S(2)}, u32[]{:S(2)}) async-start(f32[16,2,1920]{2,1,0:T(2,128)} %broadcast_in_dim.17), calls=%async_computation.5 | async-start | bytes 491520 | tf_op jit(solution)/shard_map/all_to_all | solution.py:14
  187.7 284.0 %all-reduce.2.cloned.1.call-start = ((), (), s32[]{:S(2)}) async-start(), calls=%async_computation.7 | async-start | bytes 933888 | tf_op jit(solution)/shard_map/psum | solution.py:140
  216.6 289.9 %all-to-all-start.6 = ((f32[16,128,300]{1,2,0:T(8,128)}), f32[16,128,300]{1,2,0:T(8,128)S(1)}, u32[]{:S(2)}, u32[]{:S(2)}) async-start(f32[16,128,300]{1,2,0:T(8,128)} %copy.60), calls=%async_computation.6 | async-start | bytes 4980736 | tf_op jit(solution)/shard_map/all_to_all | solution.py:86
  478.8 26.8 %copy-start = (bf16[128,300]{0,1:T(8,128)(2,1)S(1)}, bf16[128,300]{0,1:T(8,128)(2,1)}, u32[]{:S(2)}) copy-start(bf16[128,300]{0,1:T(8,128)(2,1)} %param.2) | copy-start | bytes 230404
Sparse Core Ops, SparseCore 0:
  212.2 259.4 all-reduce.1
where the time goes:
time: 523 us; the launch traced here: 515 us
  waiting for transfers between devices  287 us (55%)
  blocking collectives  64.2 us (12%)
  other arithmetic  55 us (11%)
  matrix products  53.5 us (10%)
  starting transfers between devices  21.3 us (4%)
  local copies, waits for them, and re-layouts  18.1 us (3%)
  between operations  15.8 us (3%)
    psum x1, waiting for transfers between devices, body(): cov = lax.psum(term, ('src', 'tgt'))  248 us
    all_to_all x4, blocking collectives, sent_to_all(): return lax.all_to_all(copies, axis, split_axis=0, concat_axis=0, tiled=True)  64.2 us
    all_to_all x2, waiting for transfers between devices, sent_to_all(): return lax.all_to_all(copies, axis, split_axis=0, concat_axis=0, tiled=True)  38.7 us
    dot_general x12, matrix products, body(): jnp.dot(ortho, jnp.dot(ortho.T, ortho, precision=highest), precision=high...  16.4 us
    reduce_sum x2, other arithmetic, body(): jnp.sum(jnp.exp(logits - col_top[None, :]), axis=0)  16.2 us
    reduce_sum x2, other arithmetic, body(): jnp.sum(jnp.exp(row_logits - higher[:, None]), axis=1)  15.8 us
    all_to_all x2, starting transfers between devices, sent_to_all(): return lax.all_to_all(copies, axis, split_axis=0, concat_axis=0, tiled=True)  14.7 us
    dot_general x12, matrix products, body(): jnp.dot(ortho.T, ortho, precision=highest)  13.8 us
  transfers between devices with their start and end apart: 4, of which 3 were waited for; matrix products, arithmetic and copies ran while one was open for 8% of the time, Pallas kernels for 0%

commit v1 on v0

v1 whole, which is shorter than its diff:
```python
import math

import jax
import jax.numpy as jnp
from jax import lax
from jax.experimental import pallas as pl
from jax.experimental.pallas import tpu as pltpu
from jax.sharding import PartitionSpec as P

MESH = pl.DeviceIdType.MESH
F32 = jnp.float32
BF16 = jnp.bfloat16
ITERS = 2
NEWTON = 12
EXACT_STEPS = 3
LN2 = math.log(2.0)
NEG = -1e30
D = 300
DP = 384
DR = 304
NT_OWN = 120


def remote(src, dst, send, recv, device):
    return pltpu.make_async_remote_copy(
        src_ref=src, dst_ref=dst, send_sem=send, recv_sem=recv, device_id=device, device_id_type=MESH
    )


def nt(a, b):
    return lax.dot_general(a, b, (((1,), (1,)), ((), ())), preferred_element_type=F32)


def nn(a, b):
    return jnp.dot(a, b, preferred_element_type=F32)


def split(v):
    hi = v.astype(BF16)
    return hi, (v - hi.astype(F32)).astype(BF16)


def kernel(
    src_ref, tgt_ref, rot_ref, mat_ref, ort_ref, rp_ref, cp_ref,
    s_all, t_all, s_t, logit, rexp, cexp, dense, cmax, csum, rpot, cpot,
    row_out, row_in, col_out, col_in,
    plan, summed, pair_out, pair_in, z_out, z_in,
    cacc, cov_out, cov_pair, rs_out, rs_in, zc_out, zc_in, full, x_ref,
    s_send, s_recv, f_send, t_send, t_recv, row_send, row_recv, col_send, col_recv,
    pair_send, pair_recv, z_send, z_recv, cv_send, cv_recv, rs_send, rs_recv,
    zc_send, zc_recv, ag_send, ag_recv, hf_send, hf_recv,
):
    si = lax.axis_index("src")
    ti = lax.axis_index("tgt")
    x_hi, z = si // 8, si % 8
    x_lo, y, core = ti // 8, (ti // 2) % 4, ti % 2
    other = 1 - core
    g = z * 2 + core
    h = (x_hi * 2 + x_lo) * 4 + y
    partner = (si, x_lo * 8 + y * 2 + other)

    def z_dev(p):
        return (x_hi * 8 + p, ti)

    def s_dev(p):
        return (x_hi * 8 + p // 2, x_lo * 8 + y * 2 + p % 2)

    def t_dev(p):
        return ((p // 8) * 8 + z, ((p // 4) % 2) * 8 + (p % 4) * 2 + core)

    def each(lo, hi, body):
        def step(k, carry):
            body(k)
            return carry
        lax.fori_loop(lo, hi, step, 0)

    s_all[pl.ds(g, 1)] = jnp.zeros((1, 128, DP), BF16)
    t_all[pl.ds(h, 1)] = jnp.zeros((1, 128, DP), BF16)
    s_all[g, :, 0:D] = src_ref[...]
    t_all[h, 0:NT_OWN, 0:D] = tgt_ref[...]

    barrier = pltpu.get_barrier_semaphore()

    def greet(k):
        pl.semaphore_signal(barrier, inc=1, device_id=s_dev((g + k) % 16), device_id_type=MESH)
        pl.semaphore_signal(barrier, inc=1, device_id=t_dev((h + k) % 16), device_id_type=MESH)

    each(1, 16, greet)
    pl.semaphore_wait(barrier, 30)

    def s_copy(k):
        p = (z + k) % 8
        return remote(s_all.at[g], s_all.at[g], s_send.at[k], s_recv.at[g], z_dev(p))

    def s_in(p):
        return remote(s_all.at[p], s_all.at[p], s_send.at[0], s_recv.at[p], partner)

    def forward(p):
        return remote(s_all.at[p], s_all.at[p], f_send.at[p // 2], s_recv.at[p], partner)

    def t_copy(k):
        return remote(t_all.at[h], t_all.at[h], t_send.at[k], t_recv.at[h], t_dev((h + k) % 16))

    def t_in(p):
        return remote(t_all.at[p], t_all.at[p], t_send.at[0], t_recv.at[p], partner)

    forward(g).start()
    each(1, 8, lambda k: s_copy(k).start())
    each(1, 16, lambda k: t_copy(k).start())

    lane = lax.broadcasted_iota(jnp.int32, (8, 128), 1)
    padded = lane >= NT_OWN
    for j in range(16):
        cexp[:, j * 128:(j + 1) * 128] = jnp.where(padded, NEG, 0.0)
    dense[...] = jnp.zeros((128, 128), F32)
    x_ref[...] = jnp.zeros((DP, DP), F32)
    cacc[...] = jnp.zeros((DR, DP), F32)
    cov_out[...] = jnp.zeros(cov_out.shape, F32)

    def relay(k):
        p = ((z + k) % 8) * 2 + core
        s_in(p).wait_recv()
        forward(p).start()

    each(1, 8, relay)
    each(0, 8, lambda k: s_in(k * 2 + other).wait_recv())
    each(1, 16, lambda k: t_in((h + k) % 16).wait_recv())

    scale = 4.0 / math.sqrt(D) / LN2

    def multiply(q):
        piece = t_all[pl.ds(q * 2, 2)].reshape(256, DP)
        at = pl.multiple_of(q * 256, 256)
        for r in range(4):
            rows = s_all[4 * r:4 * r + 4].reshape(512, DP)
            logit[512 * r:512 * r + 512, pl.ds(at, 256)] = nt(rows, piece) * scale

    each(0, 8, multiply)

    def row_pass():
        def block(b):
            for i in range(16):
                v = logit[pl.ds(pl.multiple_of(b * 128 + 8 * i, 8), 8), :] + cexp[...]
                m = jnp.max(v, axis=1, keepdims=True)
                s = jnp.sum(jnp.exp2(v - m), axis=1, keepdims=True)
                lse = m + jnp.log2(s)
                dense[8 * i:8 * i + 8, :] = jnp.where(lane == b, lse, dense[8 * i:8 * i + 8, :])
        each(0, 16, block)

    def col_pass():
        cmax[...] = jnp.full((8, 2048), -3e38, F32)
        csum[...] = jnp.zeros((8, 2048), F32)

        def block(b):
            rows = pl.ds(pl.multiple_of(b * 128, 128), 128)
            for j in range(16):
                cols = slice(j * 128, (j + 1) * 128)
                v = (logit[rows, cols] + rexp[rows, :]).reshape(16, 8, 128)
                old = cmax[:, cols]
                m = jnp.maximum(old, jnp.max(v, axis=0))
                csum[:, cols] = csum[:, cols] * jnp.exp2(old - m) + jnp.sum(jnp.exp2(v - m[None]), axis=0)
                cmax[:, cols] = m
        each(0, 16, block)

    def exchange(out, into, send, recv, me, dev, n):
        each(1, n, lambda k: remote(out, into.at[me], send.at[k], recv.at[me], dev((me + k) % n)).start())
        into[pl.ds(me, 1)] = out[...][None]

        def arrive(k):
            c = remote(out, into.at[(me + k) % n], send.at[k], recv.at[(me + k) % n], dev((me + k) % n))
            c.wait_recv()
            c.wait_send()
        each(1, n, arrive)

    def combined(into):
        a = into[...]
        m = jnp.max(a, axis=0)
        return -(m + jnp.log2(jnp.sum(jnp.exp2(a - m[None]), axis=0)))

    for it in range(ITERS):
        row_pass()
        row_out[it] = dense[...].T[0:16, :]
        exchange(row_out.at[it], row_in.at[it], row_send.at[it], row_recv.at[it], g, s_dev, 16)
        rpot[...] = combined(row_in.at[it])
        dense[0:16, :] = rpot[...]
        turned = dense[...].T
        for b in range(16):
            rexp[b * 128:(b + 1) * 128, :] = jnp.broadcast_to(turned[:, b:b + 1], (128, 128))
        col_pass()
        top = jnp.max(cmax[...], axis=0, keepdims=True)
        whole = jnp.sum(csum[...] * jnp.exp2(cmax[...] - top), axis=0, keepdims=True)
        lse = top + jnp.log2(whole)
        for j in range(16):
            col_out[it, j:j + 1, :] = lse[:, j * 128:(j + 1) * 128]
        exchange(col_out.at[it], col_in.at[it], col_send.at[it], col_recv.at[it], h, t_dev, 16)
        cpot[...] = combined(col_in.at[it])
        for j in range(16):
            cexp[:, j * 128:(j + 1) * 128] = jnp.where(
                padded, NEG, jnp.broadcast_to(cpot[j:j + 1, :], (8, 128))
            )

    rp_ref[...] = rpot[pl.ds(g, 1), :] * LN2
    cp_ref[...] = cpot[pl.ds(h, 1), :] * LN2

    for b in range(16):
        s_t[:, b * 128:(b + 1) * 128] = s_all[b].T

    targets = t_all.reshape(2048, DP)

    def plan_chunk(r):
        def block(b):
            local = pl.ds(pl.multiple_of(b * 128, 128), 128)
            rows = pl.ds(pl.multiple_of(r * 512 + b * 128, 128), 128)
            for j in range(16):
                cols = slice(j * 128, (j + 1) * 128)
                v = logit[rows, cols] + rexp[rows, :] + cexp[0:1, cols]
                plan[local, cols] = jnp.exp2(v).astype(BF16)
        each(0, 4, block)
        piece = nn(plan[...], targets[...])
        summed[pl.ds(r * 4, 4)] = piece.reshape(4, 128, DP)
        hi, lo = split(piece)
        left = s_t[0:DR, pl.ds(pl.multiple_of(r * 512, 512), 512)]
        cacc[...] += nn(left, hi) + nn(left, lo)

    each(0, 4, plan_chunk)

    for half in range(2):
        for l in range(3):
            for r in range(19):
                at = half * 152 + r * 8
                cov_out[half, l * 19 + r] = cacc[at:at + 8, l * 128:(l + 1) * 128]
    cv = remote(cov_out.at[other], cov_pair, cv_send, cv_recv, partner)
    cv.start()

    for p in range(8):
        pair_out[p:p + 1] = summed[pl.ds(2 * p + other, 1)].astype(BF16)
    pr = remote(pair_out, pair_in, pair_send, pair_recv, partner)

    cv.wait()
    pr.start()
    rs_out[...] = (cov_out[pl.ds(core, 1)].reshape(64, 8, 128) + cov_pair[...]).reshape(16, 4, 8, 128)
    each(1, 16, lambda k: remote(
        rs_out.at[(h + k) % 16], rs_in.at[h], rs_send.at[k], rs_recv.at[h], t_dev((h + k) % 16)).start())
    rs_in[pl.ds(h, 1)] = rs_out[pl.ds(h, 1)]

    pr.wait()
    for p in range(8):
        both = summed[pl.ds(2 * p + core, 1)] + pair_in[p:p + 1].astype(F32)
        z_out[p:p + 1] = both.astype(BF16)

    def rs_arrive(k):
        p = (h + k) % 16
        c = remote(rs_out.at[p], rs_in.at[p], rs_send.at[k], rs_recv.at[p], t_dev(p))
        c.wait_recv()
        c.wait_send()
    each(1, 16, rs_arrive)
    zc_out[...] = jnp.sum(rs_in[...], axis=0)
    exchange(zc_out, zc_in, zc_send, zc_recv, z, z_dev, 8)
    mine = jnp.sum(zc_in[...], axis=0)
    full[pl.ds(core, 1), pl.ds(h, 1)] = mine[None, None]

    def ag_copy(k, p):
        return remote(full.at[core, h], full.at[core, h], ag_send.at[k], ag_recv.at[h], t_dev(p))

    each(1, 16, lambda k: ag_copy(k, (h + k) % 16).start())

    def z_copy(k):
        p = (z + k) % 8
        return remote(z_out.at[p], z_in.at[z], z_send.at[k], z_recv.at[z], z_dev(p))
    each(1, 8, lambda k: z_copy(k).start())

    def ag_arrive(k):
        p = (h + k) % 16
        c = remote(full.at[core, p], full.at[core, p], ag_send.at[k], ag_recv.at[p], t_dev(p))
        c.wait_recv()
        c.wait_send()
    each(1, 16, ag_arrive)
    hf = remote(full.at[core], full.at[core], hf_send, hf_recv, partner)
    hf.start()
    hf.wait_send()
    remote(full.at[other], full.at[other], hf_send, hf_recv, partner).wait_recv()

    for half in range(2):
        for l in range(3):
            for r in range(19):
                t = l * 19 + r
                at = half * 152 + r * 8
                x_ref[at:at + 8, l * 128:(l + 1) * 128] = full[half, t // 4, t % 4]

    cov = x_ref[...]
    square = jnp.sum(jnp.sum(cov * cov, axis=0, keepdims=True), axis=1, keepdims=True)
    x_ref[...] = cov / jnp.sqrt(square + 1e-06)
    eye = (
        lax.broadcasted_iota(jnp.int32, (DR, DP), 0) == lax.broadcasted_iota(jnp.int32, (DR, DP), 1)
    ).astype(F32)

    def newton(k):
        v = x_ref[...]
        b = v.astype(BF16)
        rest = (0.5 * (eye - nt(b[0:DR], b))).astype(BF16)
        x_ref[0:DR, :] = v[0:DR] + nn(rest, b)

    def newton_exact(k):
        v = x_ref[...]
        hi, lo = split(v)
        gram = nt(hi[0:DR], hi) + (nt(hi[0:DR], lo) + nt(lo[0:DR], hi))
        rest_hi, rest_lo = split(0.5 * (eye - gram))
        x_ref[0:DR, :] = v[0:DR] + (nn(rest_hi, hi) + (nn(rest_hi, lo) + nn(rest_lo, hi)))

    each(0, NEWTON - EXACT_STEPS, newton)
    each(0, EXACT_STEPS, newton_exact)

    ort_ref[...] = x_ref[0:D, 0:D]
    hi, lo = split(x_ref[...])
    own = s_all[pl.ds(g, 1)].reshape(128, DP)
    rot_ref[...] = (nn(own, hi) + nn(own, lo))[:, 0:D].astype(BF16)

    def z_arrive(k):
        p = (z + k) % 8
        c = remote(z_out.at[p], z_in.at[p], z_send.at[k], z_recv.at[p], z_dev(p))
        c.wait_recv()
        c.wait_send()
    each(1, 8, z_arrive)
    total = summed[pl.ds(g, 1)].reshape(128, DP) + pair_in[pl.ds(z, 1)].reshape(128, DP).astype(F32)
    for k in range(1, 8):
        total = total + z_in[pl.ds((z + k) % 8, 1)].reshape(128, DP).astype(F32)
    mat_ref[...] = total[:, 0:D]

    forward(g).wait_send()
    each(1, 8, lambda k: s_copy(k).wait_send())
    each(1, 8, lambda k: forward(((z + k) % 8) * 2 + core).wait_send())
    each(1, 16, lambda k: t_copy(k).wait_send())


def body(source_words, target_words):
    dma = pltpu.SemaphoreType.DMA
    vmem = pl.BlockSpec(memory_space=pltpu.VMEM)
    rot, mat, ort, rp, cp = pl.pallas_call(
        kernel,
        out_shape=(
            jax.ShapeDtypeStruct((128, D), BF16),
            jax.ShapeDtypeStruct((128, D), F32),
            jax.ShapeDtypeStruct((D, D), F32),
            jax.ShapeDtypeStruct((1, 128), F32),
            jax.ShapeDtypeStruct((1, 128), F32),
        ),
        in_specs=[vmem, vmem],
        out_specs=(vmem,) * 5,
        scratch_shapes=[
            pltpu.VMEM((16, 128, DP), BF16),
            pltpu.VMEM((16, 128, DP), BF16),
            pltpu.VMEM((DP, 2048), BF16),
            pltpu.VMEM((2048, 2048), F32),
            pltpu.VMEM((2048, 128), F32),
            pltpu.VMEM((8, 2048), F32),
            pltpu.VMEM((128, 128), F32),
            pltpu.VMEM((8, 2048), F32),
            pltpu.VMEM((8, 2048), F32),
            pltpu.VMEM((16, 128), F32),
            pltpu.VMEM((16, 128), F32),
            pltpu.VMEM((ITERS, 16, 128), F32),
            pltpu.VMEM((ITERS, 16, 16, 128), F32),
            pltpu.VMEM((ITERS, 16, 128), F32),
            pltpu.VMEM((ITERS, 16, 16, 128), F32),
            pltpu.VMEM((512, 2048), BF16),
            pltpu.VMEM((16, 128, DP), F32),
            pltpu.VMEM((8, 128, DP), BF16),
            pltpu.VMEM((8, 128, DP), BF16),
            pltpu.VMEM((8, 128, DP), BF16),
            pltpu.VMEM((8, 128, DP), BF16),
            pltpu.VMEM((DR, DP), F32),
            pltpu.VMEM((2, 64, 8, 128), F32),
            pltpu.VMEM((64, 8, 128), F32),
            pltpu.VMEM((16, 4, 8, 128), F32),
            pltpu.VMEM((16, 4, 8, 128), F32),
            pltpu.VMEM((4, 8, 128), F32),
            pltpu.VMEM((8, 4, 8, 128), F32),
            pltpu.VMEM((2, 16, 4, 8, 128), F32),
            pltpu.VMEM((DP, DP), F32),
            dma((8,)), dma((16,)), dma((8,)), dma((16,)), dma((16,)),
            dma((ITERS, 16)), dma((ITERS, 16)), dma((ITERS, 16)), dma((ITERS, 16)),
            dma, dma, dma((8,)), dma((8,)), dma, dma, dma((16,)), dma((16,)),
            dma((8,)), dma((8,)), dma((16,)), dma((16,)), dma, dma,
        ],
        compiler_params=pltpu.CompilerParams(
            collective_id=0, has_side_effects=True, vmem_limit_bytes=60 * 1024 * 1024
        ),
    )(source_words, target_words)
    return rot, mat, ort, rp.reshape(128), cp[0, 0:NT_OWN]


def solution(mesh):
    in_specs = (P(("src", "tgt"), None), P(("tgt", "src"), None))
    out_specs = (
        P(("src", "tgt"), None),
        P(("src", "tgt"), None),
        P(),
        P(("src", "tgt")),
        P(("tgt", "src")),
    )
    return jax.shard_map(body, mesh=mesh, in_specs=in_specs, out_specs=out_specs, check_vma=False)
```

time: 523 us -> 140 us (0.27); the launches traced: 515 us -> 140 us
  waiting for transfers between devices: 287 us -> 0 us
  Pallas kernels: 0 us -> 131 us
  blocking collectives: 64.2 us -> 0 us
  other arithmetic: 55 us -> 0 us
  matrix products: 53.5 us -> 0 us
  starting transfers between devices: 21.3 us -> 0 us
  between operations: 15.8 us -> 0.66 us
  local copies, waits for them, and re-layouts: 18.1 us -> 8.22 us
    psum x1 -> x0, waiting for transfers between devices: 248 us -> none  [body(): cov = lax.psum(term, ('src', 'tgt'))]
    pallas_call x0 -> x1, Pallas kernels: none -> 131 us  [body(): pl.pallas_call(kernel, out_shape=(jax.ShapeDtypeStruct((128, D), BF16), j...]
    all_to_all x4 -> x0, blocking collectives: 64.2 us -> none  [sent_to_all(): return lax.all_to_all(copies, axis, split_axis=0, concat_axis=0, tiled=True)]
    dot_general x28 -> x0, matrix products: 53.5 us -> none  [the longest x12 16.4 us: body(): jnp.dot(ortho, jnp.dot(ortho.T, ortho, precision=highest), precision=high...]
    all_to_all x3 -> x0, waiting for transfers between devices: 38.7 us -> none  [the longest x2 38.7 us: sent_to_all(): return lax.all_to_all(copies, axis, split_axis=0, concat_axis=0, tiled=True)]
    reduce_sum x6 -> x0, other arithmetic: 34.5 us -> none  [the longest x2 16.2 us: body(): jnp.sum(jnp.exp(logits - col_top[None, :]), axis=0)]
    all_to_all x3 -> x0, starting transfers between devices: 21.3 us -> none  [the longest x2 14.7 us: sent_to_all(): return lax.all_to_all(copies, axis, split_axis=0, concat_axis=0, tiled=True)]
    reduce_max x3 -> x0, other arithmetic: 19.7 us -> none  [the longest x2 13.1 us: body(): col_top = jnp.max(logits, axis=0)]
  transfers between devices with their start and end apart: 4 -> 0, of which waited for: 3 -> 0; matrix products, arithmetic and copies ran while one was open for 8% -> 0% of each run, Pallas kernels for 0% -> 0%
where the time goes in v1:
time: 140 us
  Pallas kernels  131 us (94%)
  local copies, waits for them, and re-layouts  8.22 us (6%)
    pallas_call x1, Pallas kernels, body(): pl.pallas_call(kernel, out_shape=(jax.ShapeDtypeStruct((128, D), BF16), j...  131 us
    unnamed x12, local copies, waits for them, and re-layouts  7.09 us

profile of v1, /device:TPU:1, one launch (start us, length us, event | category | flops | bytes accessed | tf_op | source)
XLA Modules:
  0.0 139.8 jit_solution(5291952603001022269)
XLA Ops:
  0.6 0.0 copy-start.1
  0.6 1.7 %copy.8.tgt_ref = bf16[120,300]{1,0:T(8,128)(2,1)} copy(bf16[120,300]{0,1:T(8,128)(2,1)} %param.3) | data formatting | bytes 144000 | tf_op args[1]
  2.3 0.0 copy-done.1
  2.3 0.8 copy.7.src_ref
  3.1 130.9 %shard_map.65 = (bf16[128,300]{1,0:T(8,128)(2,1)}, f32[128,300]{1,0:T(8,128)}, f32[300,300]{1,0:T(8,128)}, f32[1,128]{1,0:T(1,128)}, f32[1,128]{1,0:T(1,128)}) custom-call(bf16[128,300]{1,0:T(8,128)(2,1)} %copy.7.src_ref, bf16[120,300]{1,0:T(8,128)(2,1)} %copy.8.tgt_ref), custom_call_target="tpu_custom_call" | custom-call | tf_op jit(solution)/shard_map/pallas_call | solution.py:338
  134.0 0.0 copy-start
  134.0 1.7 %copy.9 = bf16[128,300]{0,1:T(8,128)(2,1)} copy(bf16[128,300]{1,0:T(8,128)(2,1)} %get-tuple-element.15) | data formatting | bytes 153600
  135.7 1.1 slice_bitcast_fusion
  136.8 1.7 %copy.10 = f32[128,300]{0,1:T(8,128)} copy(f32[128,300]{1,0:T(8,128)} %get-tuple-element.16) | data formatting | bytes 307200
  138.5 0.0 copy-done
  138.5 0.0 copy-start.2
  138.5 0.8 copy.13
  139.3 0.0 copy-done.2
  139.3 0.5 copy.14
Async XLA Ops:
  0.6 1.7 %copy-start.1 = (bf16[128,300]{0,1:T(8,128)(2,1)S(1)}, bf16[128,300]{0,1:T(8,128)(2,1)}, u32[]{:S(2)}) copy-start(bf16[128,300]{0,1:T(8,128)(2,1)} %param.2) | copy-start | bytes 230404
  134.0 4.5 %copy-start = (f32[300,300]{1,0:T(8,128)S(1)}, f32[300,300]{1,0:T(8,128)}, u32[]{:S(2)}) copy-start(f32[300,300]{1,0:T(8,128)} %get-tuple-element.27) | copy-start | bytes 1080004
  138.5 0.8 copy-start.2

commit v2 on v1

v2 whole, which is shorter than its diff:
```python
import math

import jax
import jax.numpy as jnp
from jax import lax
from jax.experimental import pallas as pl
from jax.experimental.pallas import tpu as pltpu
from jax.sharding import PartitionSpec as P

MESH = pl.DeviceIdType.MESH
F32 = jnp.float32
BF16 = jnp.bfloat16
ITERS = 2
NEWTON = 12
EXACT_STEPS = 2
LN2 = math.log(2.0)
NEG = -1e30
D = 300
DP = 384
DR = 304
NT_OWN = 120
HALVES = ((0, 160), (160, 144))


def remote(src, dst, send, recv, device):
    return pltpu.make_async_remote_copy(
        src_ref=src, dst_ref=dst, send_sem=send, recv_sem=recv, device_id=device, device_id_type=MESH
    )


def nt(a, b):
    return lax.dot_general(a, b, (((1,), (1,)), ((), ())), preferred_element_type=F32)


def nn(a, b):
    return jnp.dot(a, b, preferred_element_type=F32)


def split(v):
    hi = v.astype(BF16)
    return hi, (v - hi.astype(F32)).astype(BF16)


def kernel(
    src_ref, tgt_ref, rot_ref, mat_ref, ort_ref, rp_ref, cp_ref,
    s_all, t_all, t_nat, logit, cexp, rrow, dense, rmax, rsum, lmax, lsum, rpot, cpot,
    row_out, row_in, col_out, col_in,
    plan, summed, pair_out, pair_in, z_out, z_in,
    cacc, cov_out, cov_pair, rs_out, rs_in, zc_out, zc_in, full, x_ref,
    s_send, s_recv, f_send, f_recv, t_send, t_recv, th_recv, row_send, row_recv, col_send, col_recv,
    pair_send, pair_recv, z_send, z_recv, cv_send, cv_recv, rs_send, rs_recv,
    zc_send, zc_recv, ag_send, ag_recv, hf_send, hf_recv,
):
    si = lax.axis_index("src")
    ti = lax.axis_index("tgt")
    x_hi, z = si // 8, si % 8
    x_lo, y, core = ti // 8, (ti // 2) % 4, ti % 2
    other = 1 - core
    g = z * 2 + core
    h = (x_hi * 2 + x_lo) * 4 + y
    partner = (si, x_lo * 8 + y * 2 + other)

    def z_dev(p):
        return (x_hi * 8 + p, ti)

    def s_dev(p):
        return (x_hi * 8 + p // 2, x_lo * 8 + y * 2 + p % 2)

    def t_dev(p):
        return ((p // 8) * 8 + z, ((p // 4) % 2) * 8 + (p % 4) * 2 + core)

    def each(lo, hi, body):
        def step(k, carry):
            body(k)
            return carry
        lax.fori_loop(lo, hi, step, 0)

    s_all[pl.ds(g, 1)] = jnp.zeros((1, DR, 128), BF16)
    t_all[pl.ds(h, 1)] = jnp.zeros((1, DR, 128), BF16)
    s_all[g, 0:D, :] = src_ref[...]
    t_all[h, 0:D, 0:NT_OWN] = tgt_ref[...]

    barrier = pltpu.get_barrier_semaphore()

    def greet(k):
        pl.semaphore_signal(barrier, inc=1, device_id=s_dev((g + k) % 16), device_id_type=MESH)
        pl.semaphore_signal(barrier, inc=1, device_id=t_dev((h + k) % 16), device_id_type=MESH)

    each(1, 16, greet)
    lane = lax.broadcasted_iota(jnp.int32, (8, 128), 1)
    dense[...] = jnp.zeros((128, 128), F32)
    plan[...] = jnp.zeros((2048, 512), BF16)
    x_ref[...] = jnp.zeros((DP, DP), F32)
    cacc[...] = jnp.zeros((DR, DP), F32)
    cov_out[...] = jnp.zeros(cov_out.shape, F32)
    t_nat[pl.ds(h, 1)] = t_all[h].T[None]
    pl.semaphore_wait(barrier, 30)

    def part(slot, half):
        return s_all.at[slot, pl.ds(HALVES[half][0], HALVES[half][1])]

    def s_hop(way, step, half):
        origin = (z + 8 - step) % 8 if way == 0 else (z + step) % 8
        to = (z + 1) % 8 if way == 0 else (z + 7) % 8
        return remote(
            part(origin * 2 + core, half), part(origin * 2 + core, half),
            s_send.at[way, step, half], s_recv.at[origin, half], z_dev(to)
        )

    def s_wait(way, step, half):
        origin = (z + 8 - step) % 8 if way == 0 else (z + step) % 8
        slot = origin * 2 + core
        remote(part(slot, half), part(slot, half), s_send.at[0, 0, 0], s_recv.at[origin, half], partner).wait_recv()

    def hand(p):
        slot = p * 2 + core
        return remote(s_all.at[slot], s_all.at[slot], f_send.at[p], f_recv.at[p], partner)

    def handed(p):
        slot = p * 2 + other
        return remote(s_all.at[slot], s_all.at[slot], f_send.at[0], f_recv.at[p], partner)

    def place(i, j):
        return (x_hi * 2 + x_lo + i * other + j * core) % 4, (y + i * core + j * other) % 4

    def t_slot(i, j):
        px, py = place(i, j)
        return px * 4 + py

    def t_full(i, j, to_i, to_j, n):
        slot = t_slot(i, j)
        return remote(t_all.at[slot], t_all.at[slot], t_send.at[n], t_recv.at[slot], t_dev(t_slot(to_i, to_j)))

    def t_half(i, j, half, to_i, to_j, n):
        slot = t_slot(i, j)
        ref = t_all.at[slot, pl.ds(HALVES[half][0], HALVES[half][1])]
        return remote(ref, ref, t_send.at[n], th_recv.at[slot, half], t_dev(t_slot(to_i, to_j)))

    def t_wait(i, j):
        slot = t_slot(i, j)
        remote(t_all.at[slot], t_all.at[slot], t_send.at[0], t_recv.at[slot], partner).wait_recv()
        t_nat[pl.ds(slot, 1)] = t_all[slot].T[None]

    def t_wait_halves(i, j):
        slot = t_slot(i, j)
        for half in range(2):
            ref = t_all.at[slot, pl.ds(HALVES[half][0], HALVES[half][1])]
            remote(ref, ref, t_send.at[0], th_recv.at[slot, half], partner).wait_recv()
        t_nat[pl.ds(slot, 1)] = t_all[slot].T[None]

    sent = []

    def go(copy):
        copy.start()
        sent.append(copy)

    for half in range(2):
        go(s_hop(0, 0, half))
        go(s_hop(1, 0, half))
    go(t_full(0, 0, 1, 0, 0))
    go(t_full(0, 0, 3, 0, 1))
    go(t_full(0, 0, 0, 1, 2))
    go(t_full(0, 0, 0, 3, 3))
    go(hand(z))

    def s_stage(step):
        for half in range(2):
            for way in range(2):
                s_wait(way, step, half)
                if step < 3 or half == way:
                    go(s_hop(way, step, half))
        go(hand((z + 8 - step) % 8))
        go(hand((z + step) % 8))

    def spread(i, n):
        go(t_full(i, 0, 0, 1, n))
        go(t_full(i, 0, 0, 3, n + 1))

    def spread_halves(i, n):
        t_wait(i, 3)
        go(t_half(i, 3, 0, 0, 1, n))
        t_wait(i, 1)
        go(t_half(i, 1, 1, 0, 3, n + 1))

    t_wait(3, 0)
    go(t_half(3, 0, 0, 1, 0, 4))
    t_wait(1, 0)
    go(t_half(1, 0, 1, 3, 0, 5))
    spread(3, 6)
    spread(1, 8)
    s_stage(1)
    spread_halves(0, 10)
    t_wait_halves(2, 0)
    spread(2, 12)
    s_stage(2)
    spread_halves(3, 14)
    spread_halves(1, 16)
    s_stage(3)
    spread_halves(2, 18)
    far = (z + 4) % 8
    s_wait(0, 4, 0)
    s_wait(1, 4, 1)
    go(hand(far))
    for i in (0, 3, 1, 2):
        t_wait_halves(i, 2)
    each(0, 8, lambda p: handed(p).wait_recv())

    scale = 4.0 / math.sqrt(D) / LN2

    def multiply(q):
        rhs = jnp.concatenate([s_all[2 * q], s_all[2 * q + 1]], axis=1)
        at = pl.ds(pl.multiple_of(q * 256, 256), 256)
        m = jnp.full((8, 256), -3e38, F32)
        total = jnp.zeros((8, 256), F32)
        for r in range(8):
            lhs = t_nat[2 * r:2 * r + 2].reshape(256, DR)
            v = nn(lhs, rhs) * scale
            logit[256 * r:256 * r + 256, at] = v
            v = v.reshape(2, 16, 8, 256)[:, 0:NT_OWN // 8].reshape(NT_OWN // 4, 8, 256)
            old = m
            m = jnp.maximum(old, jnp.max(v, axis=0))
            total = total * jnp.exp2(old - m) + jnp.sum(jnp.exp2(v - m[None]), axis=0)
        rmax[:, at] = m
        rsum[:, at] = total

    each(0, 8, multiply)

    def row_pass():
        rmax[...] = jnp.full((8, 2048), -3e38, F32)
        rsum[...] = jnp.zeros((8, 2048), F32)

        def block(b):
            for j in range(16):
                cols = slice(j * 128, (j + 1) * 128)
                parts = []
                for c in range(2):
                    rows = pl.ds(pl.multiple_of(b * 256 + c * 128, 128), NT_OWN)
                    v = logit[rows, cols] + cexp[rows, :]
                    parts.append(v.reshape(NT_OWN // 8, 8, 128))
                old = rmax[:, cols]
                m = jnp.maximum(jnp.maximum(old, jnp.max(parts[0], axis=0)), jnp.max(parts[1], axis=0))
                rsum[:, cols] = (
                    rsum[:, cols] * jnp.exp2(old - m)
                    + jnp.sum(jnp.exp2(parts[0] - m[None]), axis=0)
                    + jnp.sum(jnp.exp2(parts[1] - m[None]), axis=0)
                )
                rmax[:, cols] = m
        each(0, 8, block)

    def col_pass():
        def block(b):
            for i in range(NT_OWN // 8):
                rows = pl.ds(pl.multiple_of(b * 128 + 8 * i, 8), 8)
                v = [
                    logit[rows, j * 128:(j + 1) * 128] + rrow[:, j * 128:(j + 1) * 128]
                    for j in range(16)
                ]
                m = v[0]
                for w in v[1:]:
                    m = jnp.maximum(m, w)
                total = jnp.exp2(v[0] - m)
                for w in v[1:]:
                    total = total + jnp.exp2(w - m)
                lmax[rows, :] = m
                lsum[rows, :] = total
        each(0, 16, block)
        for i in range(NT_OWN // 8):
            column = jnp.zeros((8, 128), F32)
            for b in range(16):
                rows = slice(b * 128 + 8 * i, b * 128 + 8 * i + 8)
                m = lmax[rows, :]
                top = jnp.max(m, axis=1, keepdims=True)
                whole = jnp.sum(lsum[rows, :] * jnp.exp2(m - top), axis=1, keepdims=True)
                column = jnp.where(lane == b, top + jnp.log2(whole), column)
            dense[8 * i:8 * i + 8, :] = column

    def exchange(out, into, send, recv, me, dev, n):
        each(1, n, lambda k: remote(out, into.at[me], send.at[k], recv.at[me], dev((me + k) % n)).start())
        into[pl.ds(me, 1)] = out[...][None]

        def arrive(k):
            c = remote(out, into.at[(me + k) % n], send.at[k], recv.at[(me + k) % n], dev((me + k) % n))
            c.wait_recv()
            c.wait_send()
        each(1, n, arrive)

    def combined(into):
        a = into[...]
        m = jnp.max(a, axis=0)
        return -(m + jnp.log2(jnp.sum(jnp.exp2(a - m[None]), axis=0)))

    for it in range(ITERS):
        if it:
            row_pass()
        top = jnp.max(rmax[...], axis=0, keepdims=True)
        whole = jnp.sum(rsum[...] * jnp.exp2(rmax[...] - top), axis=0, keepdims=True)
        lse = top + jnp.log2(whole)
        for j in range(16):
            row_out[it, j:j + 1, :] = lse[:, j * 128:(j + 1) * 128]
        exchange(row_out.at[it], row_in.at[it], row_send.at[it], row_recv.at[it], g, s_dev, 16)
        rpot[...] = combined(row_in.at[it])
        for j in range(16):
            rrow[:, j * 128:(j + 1) * 128] = jnp.broadcast_to(rpot[j:j + 1, :], (8, 128))
        col_pass()
        col_out[it] = dense[...].T[0:16, :]
        exchange(col_out.at[it], col_in.at[it], col_send.at[it], col_recv.at[it], h, t_dev, 16)
        cpot[...] = combined(col_in.at[it])
        dense[0:16, :] = cpot[...]
        turned = dense[...].T
        for b in range(16):
            cexp[b * 128:(b + 1) * 128, :] = jnp.broadcast_to(turned[:, b:b + 1], (128, 128))

    rp_ref[...] = (rpot[pl.ds(g, 1), :] * LN2).reshape(128)
    cp_ref[...] = (cpot[pl.ds(h, 1), :] * LN2)[:, 0:NT_OWN].reshape(NT_OWN)

    def plan_chunk(r):
        def block(b):
            rows = pl.ds(pl.multiple_of(b * 128, 128), NT_OWN)
            for j in range(4):
                cols = pl.ds(pl.multiple_of(r * 512 + j * 128, 128), 128)
                v = logit[rows, cols] + cexp[rows, :] + rrow[0:1, cols]
                plan[rows, j * 128:(j + 1) * 128] = jnp.exp2(v).astype(BF16)
        each(0, 16, block)
        targets = jnp.concatenate([t_all[b] for b in range(16)], axis=1)
        piece = nn(targets, plan[...])
        for j in range(4):
            summed[pl.ds(r * 4 + j, 1)] = piece[:, j * 128:(j + 1) * 128][None]
        hi, lo = split(piece)
        left = jnp.concatenate([s_all[r * 4 + j] for j in range(4)], axis=1)
        cacc[:, 0:DR] += nt(left, hi) + nt(left, lo)

    each(0, 4, plan_chunk)

    for half in range(2):
        for l in range(3):
            for r in range(19):
                at = half * 152 + r * 8
                cov_out[half, l * 19 + r] = cacc[at:at + 8, l * 128:(l + 1) * 128]
    cv = remote(cov_out.at[other], cov_pair, cv_send, cv_recv, partner)
    cv.start()

    for p in range(8):
        pair_out[p:p + 1] = summed[pl.ds(2 * p + other, 1)].astype(BF16)
    pr = remote(pair_out, pair_in, pair_send, pair_recv, partner)

    cv.wait()
    pr.start()
    rs_out[...] = (cov_out[pl.ds(core, 1)].reshape(64, 8, 128) + cov_pair[...]).reshape(16, 4, 8, 128)
    each(1, 16, lambda k: remote(
        rs_out.at[(h + k) % 16], rs_in.at[h], rs_send.at[k], rs_recv.at[h], t_dev((h + k) % 16)).start())
    rs_in[pl.ds(h, 1)] = rs_out[pl.ds(h, 1)]

    pr.wait()
    for p in range(8):
        both = summed[pl.ds(2 * p + core, 1)] + pair_in[p:p + 1].astype(F32)
        z_out[p:p + 1] = both.astype(BF16)

    def rs_arrive(k):
        p = (h + k) % 16
        c = remote(rs_out.at[p], rs_in.at[p], rs_send.at[k], rs_recv.at[p], t_dev(p))
        c.wait_recv()
        c.wait_send()
    each(1, 16, rs_arrive)
    zc_out[...] = jnp.sum(rs_in[...], axis=0)
    exchange(zc_out, zc_in, zc_send, zc_recv, z, z_dev, 8)
    mine = jnp.sum(zc_in[...], axis=0)
    full[pl.ds(core, 1), pl.ds(h, 1)] = mine[None, None]

    def ag_copy(k, p):
        return remote(full.at[core, h], full.at[core, h], ag_send.at[k], ag_recv.at[h], t_dev(p))

    each(1, 16, lambda k: ag_copy(k, (h + k) % 16).start())

    def z_copy(k):
        p = (z + k) % 8
        return remote(z_out.at[p], z_in.at[z], z_send.at[k], z_recv.at[z], z_dev(p))
    each(1, 8, lambda k: z_copy(k).start())

    def ag_arrive(k):
        p = (h + k) % 16
        c = remote(full.at[core, p], full.at[core, p], ag_send.at[k], ag_recv.at[p], t_dev(p))
        c.wait_recv()
        c.wait_send()
    each(1, 16, ag_arrive)
    hf = remote(full.at[core], full.at[core], hf_send, hf_recv, partner)
    hf.start()
    hf.wait_send()
    remote(full.at[other], full.at[other], hf_send, hf_recv, partner).wait_recv()

    for half in range(2):
        for l in range(3):
            for r in range(19):
                t = l * 19 + r
                at = half * 152 + r * 8
                x_ref[at:at + 8, l * 128:(l + 1) * 128] = full[half, t // 4, t % 4]

    cov = x_ref[...]
    square = jnp.sum(jnp.sum(cov * cov, axis=0, keepdims=True), axis=1, keepdims=True)
    x_ref[...] = cov / jnp.sqrt(square + 1e-06)
    eye = (
        lax.broadcasted_iota(jnp.int32, (DR, DP), 0) == lax.broadcasted_iota(jnp.int32, (DR, DP), 1)
    ).astype(F32)

    def newton(k):
        v = x_ref[...]
        b = v.astype(BF16)
        rest = (0.5 * (eye - nt(b[0:DR], b))).astype(BF16)
        x_ref[0:DR, :] = v[0:DR] + nn(rest, b)

    def newton_exact(k):
        v = x_ref[...]
        hi, lo = split(v)
        gram = nt(hi[0:DR], hi) + (nt(hi[0:DR], lo) + nt(lo[0:DR], hi))
        rest_hi, rest_lo = split(0.5 * (eye - gram))
        x_ref[0:DR, :] = v[0:DR] + (nn(rest_hi, hi) + (nn(rest_hi, lo) + nn(rest_lo, hi)))

    each(0, NEWTON - EXACT_STEPS, newton)
    each(0, EXACT_STEPS, newton_exact)

    ort_ref[...] = x_ref[0:D, 0:D]
    hi, lo = split(x_ref[...].T[0:DR, 0:DR])
    own = s_all[pl.ds(g, 1)].reshape(DR, 128)
    rot_ref[...] = (nn(hi, own) + nn(lo, own))[0:D, :].astype(BF16)

    def z_arrive(k):
        p = (z + k) % 8
        c = remote(z_out.at[p], z_in.at[p], z_send.at[k], z_recv.at[p], z_dev(p))
        c.wait_recv()
        c.wait_send()
    each(1, 8, z_arrive)
    total = summed[pl.ds(g, 1)].reshape(DR, 128) + pair_in[pl.ds(z, 1)].reshape(DR, 128).astype(F32)
    for k in range(1, 8):
        total = total + z_in[pl.ds((z + k) % 8, 1)].reshape(DR, 128).astype(F32)
    mat_ref[...] = total[0:D, :]

    for copy in sent:
        copy.wait_send()


def body(source_words, target_words):
    dma = pltpu.SemaphoreType.DMA
    vmem = pl.BlockSpec(memory_space=pltpu.VMEM)
    rot, mat, ort, rp, cp = pl.pallas_call(
        kernel,
        out_shape=(
            jax.ShapeDtypeStruct((D, 128), BF16),
            jax.ShapeDtypeStruct((D, 128), F32),
            jax.ShapeDtypeStruct((D, D), F32),
            jax.ShapeDtypeStruct((128,), F32),
            jax.ShapeDtypeStruct((NT_OWN,), F32),
        ),
        in_specs=[vmem, vmem],
        out_specs=(vmem,) * 5,
        scratch_shapes=[
            pltpu.VMEM((16, DR, 128), BF16),
            pltpu.VMEM((16, DR, 128), BF16),
            pltpu.VMEM((16, 128, DR), BF16),
            pltpu.VMEM((2048, 2048), F32),
            pltpu.VMEM((2048, 128), F32),
            pltpu.VMEM((8, 2048), F32),
            pltpu.VMEM((128, 128), F32),
            pltpu.VMEM((8, 2048), F32),
            pltpu.VMEM((8, 2048), F32),
            pltpu.VMEM((2048, 128), F32),
            pltpu.VMEM((2048, 128), F32),
            pltpu.VMEM((16, 128), F32),
            pltpu.VMEM((16, 128), F32),
            pltpu.VMEM((ITERS, 16, 128), F32),
            pltpu.VMEM((ITERS, 16, 16, 128), F32),
            pltpu.VMEM((ITERS, 16, 128), F32),
            pltpu.VMEM((ITERS, 16, 16, 128), F32),
            pltpu.VMEM((2048, 512), BF16),
            pltpu.VMEM((16, DR, 128), F32),
            pltpu.VMEM((8, DR, 128), BF16),
            pltpu.VMEM((8, DR, 128), BF16),
            pltpu.VMEM((8, DR, 128), BF16),
            pltpu.VMEM((8, DR, 128), BF16),
            pltpu.VMEM((DR, DP), F32),
            pltpu.VMEM((2, 64, 8, 128), F32),
            pltpu.VMEM((64, 8, 128), F32),
            pltpu.VMEM((16, 4, 8, 128), F32),
            pltpu.VMEM((16, 4, 8, 128), F32),
            pltpu.VMEM((4, 8, 128), F32),
            pltpu.VMEM((8, 4, 8, 128), F32),
            pltpu.VMEM((2, 16, 4, 8, 128), F32),
            pltpu.VMEM((DP, DP), F32),
            dma((2, 4, 2)), dma((8, 2)), dma((8,)), dma((8,)), dma((22,)), dma((16,)), dma((16, 2)),
            dma((ITERS, 16)), dma((ITERS, 16)), dma((ITERS, 16)), dma((ITERS, 16)),
            dma, dma, dma((8,)), dma((8,)), dma, dma, dma((16,)), dma((16,)),
            dma((8,)), dma((8,)), dma((16,)), dma((16,)), dma, dma,
        ],
        compiler_params=pltpu.CompilerParams(
            collective_id=0, has_side_effects=True, vmem_limit_bytes=60 * 1024 * 1024
        ),
    )(source_words.T, target_words.T)
    return rot.T, mat.T, ort, rp, cp


def solution(mesh):
    in_specs = (P(("src", "tgt"), None), P(("tgt", "src"), None))
    out_specs = (
        P(("src", "tgt"), None),
        P(("src", "tgt"), None),
        P(),
        P(("src", "tgt")),
        P(("tgt", "src")),
    )
    return jax.shard_map(body, mesh=mesh, in_specs=in_specs, out_specs=out_specs, check_vma=False)
```

time: 140 us -> 118 us (0.84)
  Pallas kernels: 131 us -> 112 us
  local copies, waits for them, and re-layouts: 8.22 us -> 5.03 us
    pallas_call x1, Pallas kernels: 131 us -> 112 us  [body(): pl.pallas_call(kernel, out_shape=(jax.ShapeDtypeStruct((D, 128), BF16), j...]
    unnamed x12 -> x11, local copies, waits for them, and re-layouts: 7.09 us -> 5.03 us
where the time goes in v2:
time: 118 us; the launch traced here: 117 us
  Pallas kernels  112 us (95%)
  local copies, waits for them, and re-layouts  5.03 us (4%)
    pallas_call x1, Pallas kernels, body(): pl.pallas_call(kernel, out_shape=(jax.ShapeDtypeStruct((D, 128), BF16), j...  112 us
    unnamed x11, local copies, waits for them, and re-layouts  5.03 us

profile of v2, /device:TPU:1, one launch (start us, length us, event | category | flops | bytes accessed | tf_op | source)
XLA Modules:
  0.0 117.5 jit_solution(12464324398280760069)
XLA Ops:
  0.6 111.8 %shard_map.65 = (bf16[300,128]{1,0:T(8,128)(2,1)}, f32[300,128]{1,0:T(8,128)}, f32[300,300]{1,0:T(8,128)}, f32[128]{0:T(128)}, f32[120]{0:T(128)}) custom-call(bf16[300,128]{1,0:T(8,128)(2,1)} %bitcast.5, bf16[300,120]{1,0:T(8,128)(2,1)} %bitcast.6), custom_call_target="tpu_custom_call" | custom-call | tf_op jit(solution)/shard_map/pallas_call | solution.py:443
  112.4 0.0 copy-start
  112.5 1.6 %copy.12 = bf16[128,300]{0,1:T(8,128)(2,1)} copy(bf16[128,300]{0,1:T(8,128)(2,1)} %bitcast.7) | data formatting | bytes 153600
  114.0 1.6 %copy.13 = f32[128,300]{0,1:T(8,128)} copy(f32[128,300]{0,1:T(8,128)} %bitcast.4) | data formatting | bytes 307200
  115.6 0.0 copy-done
  115.6 0.0 copy-start.2
  115.6 0.8 copy.14
  116.4 0.0 copy-done.2
  116.4 0.0 copy-start.1
  116.4 0.5 copy.15
  116.9 0.1 copy-done.1
  117.0 0.5 copy.16
Async XLA Ops:
  112.4 3.2 %copy-start = (f32[300,300]{1,0:T(8,128)S(1)}, f32[300,300]{1,0:T(8,128)}, u32[]{:S(2)}) copy-start(f32[300,300]{1,0:T(8,128)} %get-tuple-element.22) | copy-start | bytes 1080004
  115.6 0.8 copy-start.2
  116.4 0.6 copy-start.1

commit v3 on v2

v3 whole, which is shorter than its diff:
```python
import math

import jax
import jax.numpy as jnp
from jax import lax
from jax.experimental import pallas as pl
from jax.experimental.pallas import tpu as pltpu
from jax.sharding import PartitionSpec as P

MESH = pl.DeviceIdType.MESH
F32 = jnp.float32
BF16 = jnp.bfloat16
ITERS = 2
NEWTON = 12
EXACT_STEPS = 2
LN2 = math.log(2.0)
NEG = -1e30
D = 300
DP = 384
DR = 304
NT_OWN = 120
HALVES = ((0, 160), (160, 144))


def remote(src, dst, send, recv, device):
    return pltpu.make_async_remote_copy(
        src_ref=src, dst_ref=dst, send_sem=send, recv_sem=recv, device_id=device, device_id_type=MESH
    )


def nt(a, b):
    return lax.dot_general(a, b, (((1,), (1,)), ((), ())), preferred_element_type=F32)


def nn(a, b):
    return jnp.dot(a, b, preferred_element_type=F32)


def split(v):
    hi = v.astype(BF16)
    return hi, (v - hi.astype(F32)).astype(BF16)


def kernel(
    src_ref, tgt_ref, rot_ref, mat_ref, ort_ref, rp_ref, cp_ref,
    s_all, t_all, t_nat, logit, cexp, rrow, dense, rmax, rsum, lmax, lsum, rpot, cpot,
    row_out, row_in, col_out, col_in,
    plan, lines, summed, pair_in, z_out, z_in,
    cacc, cov_out, cov_pair, rs_out, rs_in, zc_out, zc_in, full, x_ref,
    s_send, s_recv, f_send, f_recv, t_send, t_recv, th_recv, row_send, row_recv, col_send, col_recv,
    pair_send, pair_recv, z_send, z_recv, cv_send, cv_recv, rs_send, rs_recv,
    zc_send, zc_recv, ag_send, ag_recv, hf_send, hf_recv,
):
    si = lax.axis_index("src")
    ti = lax.axis_index("tgt")
    x_hi, z = si // 8, si % 8
    x_lo, y, core = ti // 8, (ti // 2) % 4, ti % 2
    other = 1 - core
    g = z * 2 + core
    h = (x_hi * 2 + x_lo) * 4 + y
    partner = (si, x_lo * 8 + y * 2 + other)

    def z_dev(p):
        return (x_hi * 8 + p, ti)

    def s_dev(p):
        return (x_hi * 8 + p // 2, x_lo * 8 + y * 2 + p % 2)

    def t_dev(p):
        return ((p // 8) * 8 + z, ((p // 4) % 2) * 8 + (p % 4) * 2 + core)

    def each(lo, hi, body):
        def step(k, carry):
            body(k)
            return carry
        lax.fori_loop(lo, hi, step, 0)

    s_all[0] = jnp.zeros((DR, 128), BF16)
    t_all[0] = jnp.zeros((DR, 128), BF16)
    s_all[0, 0:D, :] = src_ref[...]
    t_all[0, 0:D, 0:NT_OWN] = tgt_ref[...]

    def place(i, j):
        return (x_hi * 2 + x_lo + i * other + j * core) % 4, (y + i * core + j * other) % 4

    def t_slot(i, j):
        px, py = place(i, j)
        return px * 4 + py

    barrier = pltpu.get_barrier_semaphore()
    near = [partner, z_dev((z + 1) % 8), z_dev((z + 7) % 8)]
    near += [t_dev(t_slot(*at)) for at in ((1, 0), (3, 0), (2, 0), (0, 1), (0, 3))]
    for device in near:
        pl.semaphore_signal(barrier, inc=1, device_id=device, device_id_type=MESH)
    lane = lax.broadcasted_iota(jnp.int32, (8, 128), 1)
    dense[...] = jnp.zeros((128, 128), F32)
    for b in range(16):
        plan[b * 128 + NT_OWN:(b + 1) * 128, :] = jnp.zeros((128 - NT_OWN, 2048), BF16)
    x_ref[...] = jnp.zeros((DP, DP), F32)
    cacc[...] = jnp.zeros((DR, DP), F32)
    cov_out[...] = jnp.zeros(cov_out.shape, F32)
    t_nat[0] = t_all[0].T
    rmax[...] = jnp.full((8, 2048), -3e38, F32)
    rsum[...] = jnp.zeros((8, 2048), F32)
    pl.semaphore_wait(barrier, 8)

    def part(slot, half):
        return s_all.at[slot, pl.ds(HALVES[half][0], HALVES[half][1])]

    def s_hop(way, step, half):
        here = (8 - step) % 8 if way == 0 else step
        there = (here + 7) % 8 if way == 0 else here + 1
        to = (z + 1) % 8 if way == 0 else (z + 7) % 8
        return remote(
            part(2 * here, half), part(2 * there, half),
            s_send.at[way, step, half], s_recv.at[there, half], z_dev(to)
        )

    def s_wait(way, step, half):
        k = (8 - step) % 8 if way == 0 else step
        remote(part(2 * k, half), part(2 * k, half), s_send.at[0, 0, 0], s_recv.at[k, half], partner).wait_recv()

    def hand(k):
        return remote(s_all.at[2 * k], s_all.at[2 * k + 1], f_send.at[k], f_recv.at[k], partner)

    def handed(k):
        return remote(s_all.at[2 * k], s_all.at[2 * k + 1], f_send.at[0], f_recv.at[k], partner)

    def moved(i, j, to_i, to_j):
        return ((i - to_i) % 4) * 4 + (j - to_j) % 4

    def t_full(i, j, to_i, to_j, n):
        there = moved(i, j, to_i, to_j)
        return remote(
            t_all.at[4 * i + j], t_all.at[there], t_send.at[n], t_recv.at[there], t_dev(t_slot(to_i, to_j))
        )

    def t_half(i, j, half, to_i, to_j, n):
        there = moved(i, j, to_i, to_j)
        rows = pl.ds(HALVES[half][0], HALVES[half][1])
        return remote(
            t_all.at[4 * i + j, rows], t_all.at[there, rows],
            t_send.at[n], th_recv.at[there, half], t_dev(t_slot(to_i, to_j))
        )

    def t_wait(i, j):
        slot = 4 * i + j
        remote(t_all.at[slot], t_all.at[slot], t_send.at[0], t_recv.at[slot], partner).wait_recv()
        t_nat[slot] = t_all[slot].T

    def t_wait_halves(i, j):
        slot = 4 * i + j
        for half in range(2):
            ref = t_all.at[slot, pl.ds(HALVES[half][0], HALVES[half][1])]
            remote(ref, ref, t_send.at[0], th_recv.at[slot, half], partner).wait_recv()
        t_nat[slot] = t_all[slot].T

    sent = []

    def go(copy):
        copy.start()
        sent.append(copy)

    for half in range(2):
        go(s_hop(0, 0, half))
        go(s_hop(1, 0, half))
    go(t_full(0, 0, 1, 0, 0))
    go(t_full(0, 0, 3, 0, 1))
    go(t_full(0, 0, 0, 1, 2))
    go(t_full(0, 0, 0, 3, 3))
    go(t_full(0, 0, 2, 0, 4))
    go(hand(0))

    def s_stage(step):
        for half in range(2):
            for way in range(2):
                s_wait(way, step, half)
                if step < 3 or half == way:
                    go(s_hop(way, step, half))
        go(hand(8 - step))
        go(hand(step))

    def spread(i, n):
        go(t_full(i, 0, 0, 1, n))
        go(t_full(i, 0, 0, 3, n + 1))

    def spread_halves(i, n):
        t_wait(i, 3)
        go(t_half(i, 3, 0, 0, 1, n))
        t_wait(i, 1)
        go(t_half(i, 1, 1, 0, 3, n + 1))

    scale = 4.0 / math.sqrt(D) / LN2

    def tile(p, places):
        rhs = jnp.concatenate([s_all[2 * p], s_all[2 * p + 1]], axis=1)
        at = pl.ds(pl.multiple_of(p * 256, 256), 256)
        slots = [4 * i + j for i, j in places]
        m = rmax[:, at]
        total = rsum[:, at]
        for n in range(0, len(slots), 2):
            pair = slots[n:n + 2]
            v = nn(jnp.concatenate([t_nat[slot] for slot in pair], axis=0), rhs) * scale
            parts = []
            for k, slot in enumerate(pair):
                w = v[k * 128:k * 128 + 128]
                logit[slot * 128:slot * 128 + 128, at] = w
                parts.append(w[0:NT_OWN].reshape(NT_OWN // 8, 8, 256))
            w = jnp.concatenate(parts, axis=0)
            old = m
            m = jnp.maximum(old, jnp.max(w, axis=0))
            total = total * jnp.exp2(old - m) + jnp.sum(jnp.exp2(w - m[None]), axis=0)
        rmax[:, at] = m
        rsum[:, at] = total

    def tiles(first, n, places):
        for k in range(n):
            tile((first + k) % 8, places)

    first_five = ((0, 0), (1, 0), (3, 0), (0, 1), (0, 3))
    t_wait(3, 0)
    t_wait(1, 0)
    spread(3, 6)
    spread(1, 8)
    s_stage(1)
    t_wait(2, 0)
    spread(2, 12)
    spread_halves(0, 10)
    for k in (0, 1, 7):
        handed(k).wait_recv()
    tiles(7, 3, first_five)
    s_stage(2)
    spread_halves(3, 14)
    spread_halves(1, 16)
    for k in (2, 6):
        handed(k).wait_recv()
        tile(k, first_five)
    s_stage(3)
    spread_halves(2, 18)
    ring = ((2, 0), (3, 3), (3, 1), (1, 3), (1, 1), (2, 3), (2, 1))
    tiles(6, 5, ring[0:4])
    s_wait(0, 4, 0)
    s_wait(1, 4, 1)
    go(hand(4))
    tiles(6, 5, ring[4:])
    for k in (3, 5, 4):
        handed(k).wait_recv()
        tile(k, first_five)
    tiles(3, 3, ring)
    for i in (0, 3, 1, 2):
        t_wait_halves(i, 2)
    tiles(0, 8, ((0, 2), (1, 2), (2, 2), (3, 2)))

    def row_again():
        rsum[...] = jnp.zeros((8, 2048), F32)

        def block(b):
            rows = pl.ds(pl.multiple_of(b * 128, 128), NT_OWN)
            for j in range(16):
                cols = slice(j * 128, (j + 1) * 128)
                v = jnp.exp2(logit[rows, cols] + cexp[rows, :] + rrow[0:1, cols])
                logit[rows, cols] = v
                rsum[:, cols] += jnp.sum(v.reshape(NT_OWN // 8, 8, 128), axis=0)
        each(0, 16, block)

    def col_again():
        def block(b):
            rows = pl.ds(pl.multiple_of(b * 128, 128), NT_OWN)
            total = jnp.zeros((NT_OWN, 128), F32)
            for j in range(16):
                cols = slice(j * 128, (j + 1) * 128)
                total = total + logit[rows, cols] * rrow[0:1, cols]
            lsum[rows, :] = total
        each(0, 16, block)
        for i in range(NT_OWN // 8):
            column = jnp.zeros((8, 128), F32)
            for b in range(16):
                rows = slice(b * 128 + 8 * i, b * 128 + 8 * i + 8)
                column = jnp.where(lane == b, jnp.sum(lsum[rows, :], axis=1, keepdims=True), column)
            dense[8 * i:8 * i + 8, :] = column

    def col_pass():
        def block(b):
            for i in range(NT_OWN // 8):
                rows = pl.ds(pl.multiple_of(b * 128 + 8 * i, 8), 8)
                v = [
                    logit[rows, j * 128:(j + 1) * 128] + rrow[:, j * 128:(j + 1) * 128]
                    for j in range(16)
                ]
                m = v[0]
                for w in v[1:]:
                    m = jnp.maximum(m, w)
                total = jnp.exp2(v[0] - m)
                for w in v[1:]:
                    total = total + jnp.exp2(w - m)
                lmax[rows, :] = m
                lsum[rows, :] = total
        each(0, 16, block)
        for i in range(NT_OWN // 8):
            column = jnp.zeros((8, 128), F32)
            for b in range(16):
                rows = slice(b * 128 + 8 * i, b * 128 + 8 * i + 8)
                m = lmax[rows, :]
                top = jnp.max(m, axis=1, keepdims=True)
                whole = jnp.sum(lsum[rows, :] * jnp.exp2(m - top), axis=1, keepdims=True)
                column = jnp.where(lane == b, top + jnp.log2(whole), column)
            dense[8 * i:8 * i + 8, :] = column

    def exchange(out, into, send, recv, me, dev, n):
        each(1, n, lambda k: remote(out, into.at[me], send.at[k], recv.at[me], dev((me + k) % n)).start())
        into[pl.ds(me, 1)] = out[...][None]

        def arrive(k):
            c = remote(out, into.at[(me + k) % n], send.at[k], recv.at[(me + k) % n], dev((me + k) % n))
            c.wait_recv()
            c.wait_send()
        each(1, n, arrive)

    def combined(into):
        a = into[...]
        m = jnp.max(a, axis=0)
        return -(m + jnp.log2(jnp.sum(jnp.exp2(a - m[None]), axis=0)))

    def s_order(r):
        return ((z + r // 2) % 8) * 2 + (core if r % 2 == 0 else other)

    def t_order(r):
        return t_slot(r // 4, r % 4)

    def to_rows(ref):
        for r in range(16):
            rrow[:, r * 128:(r + 1) * 128] = jnp.broadcast_to(ref[pl.ds(s_order(r), 1), :], (8, 128))

    def out_row(it, values):
        for r in range(16):
            row_out[it, pl.ds(s_order(r), 1), :] = values[:, r * 128:(r + 1) * 128]

    def out_col(it):
        lines[...] = dense[...].T[0:16, :]
        for r in range(16):
            col_out[it, pl.ds(t_order(r), 1), :] = lines[r:r + 1, :]

    def to_cols(ref):
        for r in range(16):
            dense[r:r + 1, :] = ref[pl.ds(t_order(r), 1), :]
        turned = dense[...].T
        for b in range(16):
            cexp[b * 128:(b + 1) * 128, :] = jnp.broadcast_to(turned[:, b:b + 1], (128, 128))

    top = jnp.max(rmax[...], axis=0, keepdims=True)
    whole = jnp.sum(rsum[...] * jnp.exp2(rmax[...] - top), axis=0, keepdims=True)
    out_row(0, top + jnp.log2(whole))
    exchange(row_out.at[0], row_in.at[0], row_send.at[0], row_recv.at[0], g, s_dev, 16)
    rpot[...] = combined(row_in.at[0])
    to_rows(rpot)
    col_pass()
    out_col(0)
    exchange(col_out.at[0], col_in.at[0], col_send.at[0], col_recv.at[0], h, t_dev, 16)
    cpot[...] = combined(col_in.at[0])
    to_cols(cpot)

    row_again()
    out_row(1, jnp.sum(rsum[...], axis=0, keepdims=True))
    exchange(row_out.at[1], row_in.at[1], row_send.at[1], row_recv.at[1], g, s_dev, 16)
    whole = jnp.sum(row_in[1], axis=0)
    rpot[...] = rpot[...] - jnp.log2(whole)
    lines[...] = 1.0 / whole
    to_rows(lines)
    col_again()
    out_col(1)
    exchange(col_out.at[1], col_in.at[1], col_send.at[1], col_recv.at[1], h, t_dev, 16)
    whole = jnp.sum(col_in[1], axis=0)
    cpot[...] = cpot[...] - jnp.log2(whole)
    lines[...] = 1.0 / whole
    to_cols(lines)

    rp_ref[...] = (rpot[pl.ds(g, 1), :] * LN2).reshape(128)
    cp_ref[...] = (cpot[pl.ds(h, 1), :] * LN2)[:, 0:NT_OWN].reshape(NT_OWN)

    def fill(q):
        for b in range(16):
            rows = slice(b * 128, b * 128 + NT_OWN)
            share = cexp[rows, :]
            for j in range(4):
                cols = slice(q * 512 + j * 128, q * 512 + j * 128 + 128)
                plan[rows, cols] = (logit[rows, cols] * rrow[0:1, cols] * share).astype(BF16)

    targets = jnp.concatenate([t_all[b] for b in range(16)], axis=1)
    fill(0)
    for q in range(4):
        if q < 3:
            fill(q + 1)
        piece = nn(targets, plan[:, q * 512:(q + 1) * 512])
        for j in range(4):
            summed[4 * q + j] = piece[:, j * 128:(j + 1) * 128]
        cacc[:, 0:DR] += nt(piece.astype(BF16), jnp.concatenate([s_all[4 * q + j] for j in range(4)], axis=1))

    for half in range(2):
        at = half * 152
        for r in range(19):
            for l in range(2):
                cov_out[half, l * 19 + r] = cacc[at + 8 * r:at + 8 * r + 8, l * 128:(l + 1) * 128]
        for r in range(10):
            last = cacc[at + 8 * r:at + 8 * r + 8, 256:384]
            if r < 9:
                last = last + pltpu.roll(cacc[at + 80 + 8 * r:at + 88 + 8 * r, 256:384], 64, 1)
            cov_out[half, 38 + r] = last
    cv = remote(cov_out.at[other], cov_pair, cv_send, cv_recv, partner)
    cv.start()

    pr = [
        remote(summed.at[2 * k + 1], pair_in.at[k], pair_send.at[k], pair_recv.at[k], partner) for k in range(8)
    ]

    cv.wait()
    for copy in pr:
        copy.start()
    rs_out[...] = (cov_out[pl.ds(core, 1)].reshape(48, 8, 128) + cov_pair[...]).reshape(16, 24, 128).astype(BF16)
    each(1, 16, lambda k: remote(
        rs_out.at[(h + k) % 16], rs_in.at[h], rs_send.at[k], rs_recv.at[h], t_dev((h + k) % 16)).start())
    rs_in[pl.ds(h, 1)] = rs_out[pl.ds(h, 1)]

    for k in range(1, 8):
        pr[k].wait_recv()
        z_out[k] = (summed[2 * k] + pair_in[k]).astype(BF16)

    def rs_arrive(k):
        p = (h + k) % 16
        c = remote(rs_out.at[p], rs_in.at[p], rs_send.at[k], rs_recv.at[p], t_dev(p))
        c.wait_recv()
        c.wait_send()
    each(1, 16, rs_arrive)
    zc_out[...] = jnp.sum(rs_in[...].astype(F32), axis=0).reshape(3, 8, 128)
    exchange(zc_out, zc_in, zc_send, zc_recv, z, z_dev, 8)
    mine = jnp.sum(zc_in[...], axis=0)
    full[pl.ds(core, 1), pl.ds(h, 1)] = mine[None, None]

    def ag_copy(k, p):
        return remote(full.at[core, h], full.at[core, h], ag_send.at[k], ag_recv.at[h], t_dev(p))

    each(1, 16, lambda k: ag_copy(k, (h + k) % 16).start())

    def z_copy(k):
        return remote(z_out.at[k], z_in.at[k], z_send.at[k], z_recv.at[k], z_dev((z + k) % 8))
    each(1, 8, lambda k: z_copy(k).start())

    def ag_arrive(k):
        p = (h + k) % 16
        c = remote(full.at[core, p], full.at[core, p], ag_send.at[k], ag_recv.at[p], t_dev(p))
        c.wait_recv()
        c.wait_send()
    each(1, 16, ag_arrive)
    hf = remote(full.at[core], full.at[core], hf_send, hf_recv, partner)
    hf.start()
    hf.wait_send()
    remote(full.at[other], full.at[other], hf_send, hf_recv, partner).wait_recv()

    def tile_of(half, t):
        return full[half, t // 3, t % 3]

    for half in range(2):
        at = half * 152
        for r in range(19):
            for l in range(2):
                x_ref[at + 8 * r:at + 8 * r + 8, l * 128:(l + 1) * 128] = tile_of(half, l * 19 + r)
        for r in range(10):
            last = tile_of(half, 38 + r)
            x_ref[at + 8 * r:at + 8 * r + 8, 256:384] = jnp.where(lane < 44, last, 0.0)
            if r < 9:
                x_ref[at + 80 + 8 * r:at + 88 + 8 * r, 256:384] = jnp.where(lane < 44, pltpu.roll(last, 64, 1), 0.0)

    cov = x_ref[...]
    square = jnp.sum(jnp.sum(cov * cov, axis=0, keepdims=True), axis=1, keepdims=True)
    x_ref[...] = cov / jnp.sqrt(square + 1e-06)
    eye = (
        lax.broadcasted_iota(jnp.int32, (DR, DP), 0) == lax.broadcasted_iota(jnp.int32, (DR, DP), 1)
    ).astype(F32)

    def newton(k):
        v = x_ref[...]
        b = v.astype(BF16)
        rest = (0.5 * (eye - nt(b[0:DR], b))).astype(BF16)
        x_ref[0:DR, :] = v[0:DR] + nn(rest, b)

    def newton_exact(k):
        v = x_ref[...]
        hi, lo = split(v)
        gram = nt(hi[0:DR], hi) + (nt(hi[0:DR], lo) + nt(lo[0:DR], hi))
        rest_hi, rest_lo = split(0.5 * (eye - gram))
        x_ref[0:DR, :] = v[0:DR] + (nn(rest_hi, hi) + (nn(rest_hi, lo) + nn(rest_lo, hi)))

    each(0, NEWTON - EXACT_STEPS, newton)
    each(0, EXACT_STEPS, newton_exact)

    ort_ref[...] = x_ref[...].T[0:D, 0:D]
    hi, lo = split(x_ref[0:DR, 0:DR])
    own = s_all[0]
    rot_ref[...] = (nn(hi, own) + nn(lo, own))[0:D, :].astype(BF16)

    each(1, 8, lambda k: z_copy(k).wait())
    pr[0].wait_recv()
    total = summed[0] + pair_in[0]
    for k in range(1, 8):
        total = total + z_in[k].astype(F32)
    mat_ref[...] = total[0:D, :]

    for copy in sent + pr:
        copy.wait_send()


def store(*refs):
    for given, result in zip(refs[:5], refs[5:]):
        result[...] = given[...]


def body(source_words, target_words):
    dma = pltpu.SemaphoreType.DMA
    vmem = pl.BlockSpec(memory_space=pltpu.VMEM)
    results = pl.pallas_call(
        kernel,
        out_shape=(
            jax.ShapeDtypeStruct((D, 128), BF16),
            jax.ShapeDtypeStruct((D, 128), F32),
            jax.ShapeDtypeStruct((D, D), F32),
            jax.ShapeDtypeStruct((128,), F32),
            jax.ShapeDtypeStruct((NT_OWN,), F32),
        ),
        in_specs=[vmem, vmem],
        out_specs=(vmem,) * 5,
        scratch_shapes=[
            pltpu.VMEM((16, DR, 128), BF16),
            pltpu.VMEM((16, DR, 128), BF16),
            pltpu.VMEM((16, 128, DR), BF16),
            pltpu.VMEM((2048, 2048), F32),
            pltpu.VMEM((2048, 128), F32),
            pltpu.VMEM((8, 2048), F32),
            pltpu.VMEM((128, 128), F32),
            pltpu.VMEM((8, 2048), F32),
            pltpu.VMEM((8, 2048), F32),
            pltpu.VMEM((2048, 128), F32),
            pltpu.VMEM((2048, 128), F32),
            pltpu.VMEM((16, 128), F32),
            pltpu.VMEM((16, 128), F32),
            pltpu.VMEM((ITERS, 16, 128), F32),
            pltpu.VMEM((ITERS, 16, 16, 128), F32),
            pltpu.VMEM((ITERS, 16, 128), F32),
            pltpu.VMEM((ITERS, 16, 16, 128), F32),
            pltpu.VMEM((2048, 2048), BF16),
            pltpu.VMEM((16, 128), F32),
            pltpu.VMEM((16, DR, 128), F32),
            pltpu.VMEM((8, DR, 128), F32),
            pltpu.VMEM((8, DR, 128), BF16),
            pltpu.VMEM((8, DR, 128), BF16),
            pltpu.VMEM((DR, DP), F32),
            pltpu.VMEM((2, 48, 8, 128), F32),
            pltpu.VMEM((48, 8, 128), F32),
            pltpu.VMEM((16, 24, 128), BF16),
            pltpu.VMEM((16, 24, 128), BF16),
            pltpu.VMEM((3, 8, 128), F32),
            pltpu.VMEM((8, 3, 8, 128), F32),
            pltpu.VMEM((2, 16, 3, 8, 128), F32),
            pltpu.VMEM((DP, DP), F32),
            dma((2, 4, 2)), dma((8, 2)), dma((8,)), dma((8,)), dma((22,)), dma((16,)), dma((16, 2)),
            dma((ITERS, 16)), dma((ITERS, 16)), dma((ITERS, 16)), dma((ITERS, 16)),
            dma((8,)), dma((8,)), dma((8,)), dma((8,)), dma, dma, dma((16,)), dma((16,)),
            dma((8,)), dma((8,)), dma((16,)), dma((16,)), dma, dma,
        ],
        compiler_params=pltpu.CompilerParams(
            collective_id=0, has_side_effects=True, vmem_limit_bytes=60 * 1024 * 1024
        ),
    )(source_words.T, target_words.T)
    rot, mat, ort, rp, cp = pl.pallas_call(
        store,
        out_shape=tuple(jax.ShapeDtypeStruct(r.shape, r.dtype) for r in results),
        in_specs=[vmem] * 5,
        out_specs=(vmem,) * 5,
    )(*results)
    return rot.T, mat.T, ort, rp, cp


def solution(mesh):
    in_specs = (P(("src", "tgt"), None), P(("tgt", "src"), None))
    out_specs = (
        P(("src", "tgt"), None),
        P(("src", "tgt"), None),
        P(),
        P(("src", "tgt")),
        P(("tgt", "src")),
    )
    return jax.shard_map(body, mesh=mesh, in_specs=in_specs, out_specs=out_specs, check_vma=False)
```

time: 118 us -> 99 us (0.84)
  Pallas kernels: 112 us -> 98.2 us
  local copies, waits for them, and re-layouts: 5.03 us -> 0 us
    pallas_call x1, Pallas kernels: 112 us -> 96.2 us  [body(): pl.pallas_call(kernel, out_shape=(jax.ShapeDtypeStruct((D, 128), BF16), j...]
    unnamed x11 -> x0, local copies, waits for them, and re-layouts: 5.03 us -> none
    pallas_call x0 -> x1, Pallas kernels: none -> 2.02 us  [body(): pl.pallas_call(store, out_shape=tuple((jax.ShapeDtypeStruct(r.shape, r.dt...]
where the time goes in v3:
time: 99 us; the launch traced here: 98.8 us
  Pallas kernels  98.2 us (99%)
    pallas_call x1, Pallas kernels, body(): pl.pallas_call(kernel, out_shape=(jax.ShapeDtypeStruct((D, 128), BF16), j...  96.2 us
    pallas_call x1, Pallas kernels, body(): pl.pallas_call(store, out_shape=tuple((jax.ShapeDtypeStruct(r.shape, r.dt...  2.02 us

profile of v3, /device:TPU:1, one launch (start us, length us, event | category | flops | bytes accessed | tf_op | source)
XLA Modules:
  0.0 98.8 jit_solution(17413177155725226137)
XLA Ops:
  0.6 96.2 %shard_map.65 = (bf16[300,128]{1,0:T(8,128)(2,1)}, f32[300,128]{1,0:T(8,128)}, f32[300,300]{1,0:T(8,128)}, f32[128]{0:T(128)}, f32[120]{0:T(128)}) custom-call(bf16[300,128]{1,0:T(8,128)(2,1)} %bitcast.4, bf16[300,120]{1,0:T(8,128)(2,1)} %bitcast.5), custom_call_target="tpu_custom_call" | custom-call | tf_op jit(solution)/shard_map/pallas_call | solution.py:519
  96.8 2.0 %shard_map.66 = (bf16[300,128]{1,0:T(8,128)(2,1)}, f32[300,128]{1,0:T(8,128)}, f32[300,300]{1,0:T(8,128)}, f32[128]{0:T(128)}, f32[120]{0:T(128)}) custom-call(bf16[300,128]{1,0:T(8,128)(2,1)} %get-tuple-element.15.refs_0_, f32[300,128]{1,0:T(8,128)} %get-tuple-element.16.refs_1_, f32[300,300]{1,0:T(8,128)} %get-tuple-element.17.refs_2_, ...), custom_call_target="tpu_custom_call" | custom-call | tf_op jit(solution)/shard_map/pallas_call | solution.py:572

commit v4 on v3

--- a/solution.py
+++ b/solution.py
@@ -12,7 +12,8 @@
 BF16 = jnp.bfloat16
 ITERS = 2
 NEWTON = 12
-EXACT_STEPS = 2
+SMALL_STEPS = 5
+EXACT_STEPS = 1
 LN2 = math.log(2.0)
 NEG = -1e30
 D = 300
@@ -238,15 +239,17 @@
     s_stage(3)
     spread_halves(2, 18)
     ring = ((2, 0), (3, 3), (3, 1), (1, 3), (1, 1), (2, 3), (2, 1))
-    tiles(6, 5, ring[0:4])
+    tiles(6, 5, ring)
+    for k in (3, 5):
+        handed(k).wait_recv()
+        tile(k, first_five)
     s_wait(0, 4, 0)
     s_wait(1, 4, 1)
     go(hand(4))
-    tiles(6, 5, ring[4:])
-    for k in (3, 5, 4):
-        handed(k).wait_recv()
-        tile(k, first_five)
-    tiles(3, 3, ring)
+    tile(3, ring)
+    tile(5, ring)
+    handed(4).wait_recv()
+    tile(4, first_five + ring)
     for i in (0, 3, 1, 2):
         t_wait_halves(i, 2)
     tiles(0, 8, ((0, 2), (1, 2), (2, 2), (3, 2)))
@@ -306,15 +309,26 @@
                 column = jnp.where(lane == b, top + jnp.log2(whole), column)
             dense[8 * i:8 * i + 8, :] = column
 
-    def exchange(out, into, send, recv, me, dev, n):
-        each(1, n, lambda k: remote(out, into.at[me], send.at[k], recv.at[me], dev((me + k) % n)).start())
+    z_peers = [((z + k) % 8, z_dev((z + k) % 8)) for k in (4, 3, 5, 2, 6, 1, 7)]
+    s_peers = []
+    for k in (4, 3, 5, 2, 6, 1, 7, 0):
+        for c in range(2):
+            if k or c:
+                slot = ((z + k) % 8) * 2 + (other if c else core)
+                s_peers.append((slot, s_dev(slot)))
+    t_peers = []
+    for d in sorted(range(1, 16), key=lambda d: -(min(d // 4, 4 - d // 4) + min(d % 4, 4 - d % 4))):
+        px, py = (x_hi * 2 + x_lo + d // 4) % 4, (y + d % 4) % 4
+        t_peers.append((px * 4 + py, ((px // 2) * 8 + z, (px % 2) * 8 + py * 2 + core)))
+
+    def exchange(out, into, send, recv, me, peers):
+        for n, (slot, device) in enumerate(peers):
+            remote(out, into.at[me], send.at[n], recv.at[me], device).start()
         into[pl.ds(me, 1)] = out[...][None]
-
-        def arrive(k):
-            c = remote(out, into.at[(me + k) % n], send.at[k], recv.at[(me + k) % n], dev((me + k) % n))
-            c.wait_recv()
-            c.wait_send()
-        each(1, n, arrive)
+        for n, (slot, device) in reversed(list(enumerate(peers))):
+            copy = remote(out, into.at[slot], send.at[n], recv.at[slot], device)
+            copy.wait_recv()
+            copy.wait_send()
 
     def combined(into):
         a = into[...]
@@ -350,25 +364,25 @@
     top = jnp.max(rmax[...], axis=0, keepdims=True)
     whole = jnp.sum(rsum[...] * jnp.exp2(rmax[...] - top), axis=0, keepdims=True)
     out_row(0, top + jnp.log2(whole))
-    exchange(row_out.at[0], row_in.at[0], row_send.at[0], row_recv.at[0], g, s_dev, 16)
+    exchange(row_out.at[0], row_in.at[0], row_send.at[0], row_recv.at[0], g, s_peers)
     rpot[...] = combined(row_in.at[0])
     to_rows(rpot)
     col_pass()
     out_col(0)
-    exchange(col_out.at[0], col_in.at[0], col_send.at[0], col_recv.at[0], h, t_dev, 16)
+    exchange(col_out.at[0], col_in.at[0], col_send.at[0], col_recv.at[0], h, t_peers)
     cpot[...] = combined(col_in.at[0])
     to_cols(cpot)
 
     row_again()
     out_row(1, jnp.sum(rsum[...], axis=0, keepdims=True))
-    exchange(row_out.at[1], row_in.at[1], row_send.at[1], row_recv.at[1], g, s_dev, 16)
+    exchange(row_out.at[1], row_in.at[1], row_send.at[1], row_recv.at[1], g, s_peers)
     whole = jnp.sum(row_in[1], axis=0)
     rpot[...] = rpot[...] - jnp.log2(whole)
     lines[...] = 1.0 / whole
     to_rows(lines)
     col_again()
     out_col(1)
-    exchange(col_out.at[1], col_in.at[1], col_send.at[1], col_recv.at[1], h, t_dev, 16)
+    exchange(col_out.at[1], col_in.at[1], col_send.at[1], col_recv.at[1], h, t_peers)
     whole = jnp.sum(col_in[1], axis=0)
     cpot[...] = cpot[...] - jnp.log2(whole)
     lines[...] = 1.0 / whole
@@ -416,44 +430,42 @@
     for copy in pr:
         copy.start()
     rs_out[...] = (cov_out[pl.ds(core, 1)].reshape(48, 8, 128) + cov_pair[...]).reshape(16, 24, 128).astype(BF16)
-    each(1, 16, lambda k: remote(
-        rs_out.at[(h + k) % 16], rs_in.at[h], rs_send.at[k], rs_recv.at[h], t_dev((h + k) % 16)).start())
+    for n, (slot, device) in enumerate(t_peers):
+        remote(rs_out.at[slot], rs_in.at[h], rs_send.at[n], rs_recv.at[h], device).start()
     rs_in[pl.ds(h, 1)] = rs_out[pl.ds(h, 1)]
 
     for k in range(1, 8):
         pr[k].wait_recv()
         z_out[k] = (summed[2 * k] + pair_in[k]).astype(BF16)
 
-    def rs_arrive(k):
-        p = (h + k) % 16
-        c = remote(rs_out.at[p], rs_in.at[p], rs_send.at[k], rs_recv.at[p], t_dev(p))
-        c.wait_recv()
-        c.wait_send()
-    each(1, 16, rs_arrive)
+    for n, (slot, device) in reversed(list(enumerate(t_peers))):
+        copy = remote(rs_out.at[slot], rs_in.at[slot], rs_send.at[n], rs_recv.at[slot], device)
+        copy.wait_recv()
+        copy.wait_send()
     zc_out[...] = jnp.sum(rs_in[...].astype(F32), axis=0).reshape(3, 8, 128)
-    exchange(zc_out, zc_in, zc_send, zc_recv, z, z_dev, 8)
+    exchange(zc_out, zc_in, zc_send, zc_recv, z, z_peers)
     mine = jnp.sum(zc_in[...], axis=0)
     full[pl.ds(core, 1), pl.ds(h, 1)] = mine[None, None]
 
-    def ag_copy(k, p):
-        return remote(full.at[core, h], full.at[core, h], ag_send.at[k], ag_recv.at[h], t_dev(p))
-
-    each(1, 16, lambda k: ag_copy(k, (h + k) % 16).start())
+    for n, (slot, device) in enumerate(t_peers):
+        remote(full.at[core, h], full.at[core, h], ag_send.at[n], ag_recv.at[h], device).start()
+
+    def pass_on(slot):
+        return remote(full.at[core, slot], full.at[core, slot], hf_send.at[slot], hf_recv.at[slot], partner)
+
+    pass_on(h).start()
 
     def z_copy(k):
         return remote(z_out.at[k], z_in.at[k], z_send.at[k], z_recv.at[k], z_dev((z + k) % 8))
     each(1, 8, lambda k: z_copy(k).start())
 
-    def ag_arrive(k):
-        p = (h + k) % 16
-        c = remote(full.at[core, p], full.at[core, p], ag_send.at[k], ag_recv.at[p], t_dev(p))
-        c.wait_recv()
-        c.wait_send()
-    each(1, 16, ag_arrive)
-    hf = remote(full.at[core], full.at[core], hf_send, hf_recv, partner)
-    hf.start()
-    hf.wait_send()
-    remote(full.at[other], full.at[other], hf_send, hf_recv, partner).wait_recv()
+    for n, (slot, device) in reversed(list(enumerate(t_peers))):
+        copy = remote(full.at[core, slot], full.at[core, slot], ag_send.at[n], ag_recv.at[slot], device)
+        copy.wait_recv()
+        pass_on(slot).start()
+        copy.wait_send()
+    for slot in range(16):
+        remote(full.at[other, slot], full.at[other, slot], hf_send.at[slot], hf_recv.at[slot], partner).wait_recv()
 
     def tile_of(half, t):
         return full[half, t // 3, t % 3]
@@ -476,6 +488,12 @@
         lax.broadcasted_iota(jnp.int32, (DR, DP), 0) == lax.broadcasted_iota(jnp.int32, (DR, DP), 1)
     ).astype(F32)
 
+    def newton_small(k):
+        v = x_ref[0:DR, :]
+        b = x_ref[...].astype(BF16)
+        gram = nt(b[0:DR], b).astype(BF16)
+        x_ref[0:DR, :] = 1.5 * v - 0.5 * nn(gram, b)
+
     def newton(k):
         v = x_ref[...]
         b = v.astype(BF16)
@@ -489,7 +507,8 @@
         rest_hi, rest_lo = split(0.5 * (eye - gram))
         x_ref[0:DR, :] = v[0:DR] + (nn(rest_hi, hi) + (nn(rest_hi, lo) + nn(rest_lo, hi)))
 
-    each(0, NEWTON - EXACT_STEPS, newton)
+    each(0, SMALL_STEPS, newton_small)
+    each(SMALL_STEPS, NEWTON - EXACT_STEPS, newton)
     each(0, EXACT_STEPS, newton_exact)
 
     ort_ref[...] = x_ref[...].T[0:D, 0:D]
@@ -506,6 +525,8 @@
 
     for copy in sent + pr:
         copy.wait_send()
+    for slot in range(16):
+        pass_on(slot).wait_send()
 
 
 def store(*refs):
@@ -563,7 +584,7 @@
             dma((2, 4, 2)), dma((8, 2)), dma((8,)), dma((8,)), dma((22,)), dma((16,)), dma((16, 2)),
             dma((ITERS, 16)), dma((ITERS, 16)), dma((ITERS, 16)), dma((ITERS, 16)),
             dma((8,)), dma((8,)), dma((8,)), dma((8,)), dma, dma, dma((16,)), dma((16,)),
-            dma((8,)), dma((8,)), dma((16,)), dma((16,)), dma, dma,
+            dma((8,)), dma((8,)), dma((16,)), dma((16,)), dma((16,)), dma((16,)),
         ],
         compiler_params=pltpu.CompilerParams(
             collective_id=0, has_side_effects=True, vmem_limit_bytes=60 * 1024 * 1024

time: 99 us -> 95.5 us (0.965)
  Pallas kernels: 98.2 us -> 94.8 us
    pallas_call x1, Pallas kernels: 96.2 us -> 92.7 us  [body(): pl.pallas_call(kernel, out_shape=(jax.ShapeDtypeStruct((D, 128), BF16), j...]
where the time goes in v4:
time: 95.5 us; the launch traced here: 95.4 us
  Pallas kernels  94.8 us (99%)
    pallas_call x1, Pallas kernels, body(): pl.pallas_call(kernel, out_shape=(jax.ShapeDtypeStruct((D, 128), BF16), j...  92.7 us
    pallas_call x1, Pallas kernels, body(): pl.pallas_call(store, out_shape=tuple((jax.ShapeDtypeStruct(r.shape, r.dt...  2.02 us

profile of v4, /device:TPU:1, one launch (start us, length us, event | category | flops | bytes accessed | tf_op | source)
XLA Modules:
  0.0 95.4 jit_solution(7827973984536107049)
XLA Ops:
  0.6 92.7 %shard_map.65 = (bf16[300,128]{1,0:T(8,128)(2,1)}, f32[300,128]{1,0:T(8,128)}, f32[300,300]{1,0:T(8,128)}, f32[128]{0:T(128)}, f32[120]{0:T(128)}) custom-call(bf16[300,128]{1,0:T(8,128)(2,1)} %bitcast.4, bf16[300,120]{1,0:T(8,128)(2,1)} %bitcast.5), custom_call_target="tpu_custom_call" | custom-call | tf_op jit(solution)/shard_map/pallas_call | solution.py:540
  93.4 2.0 %shard_map.66 = (bf16[300,128]{1,0:T(8,128)(2,1)}, f32[300,128]{1,0:T(8,128)}, f32[300,300]{1,0:T(8,128)}, f32[128]{0:T(128)}, f32[120]{0:T(128)}) custom-call(bf16[300,128]{1,0:T(8,128)(2,1)} %get-tuple-element.15.refs_0_, f32[300,128]{1,0:T(8,128)} %get-tuple-element.16.refs_1_, f32[300,300]{1,0:T(8,128)} %get-tuple-element.17.refs_2_, ...), custom_call_target="tpu_custom_call" | custom-call | tf_op jit(solution)/shard_map/pallas_call | solution.py:593

commit v5 on v4

--- a/solution.py
+++ b/solution.py
@@ -233,26 +233,31 @@
     s_stage(2)
     spread_halves(3, 14)
     spread_halves(1, 16)
+    ring = ((2, 0), (3, 3), (3, 1), (1, 3), (1, 1), (2, 3), (2, 1))
+    last = ((0, 2), (1, 2), (2, 2), (3, 2))
+    tiles(7, 3, ring[0:5])
     for k in (2, 6):
         handed(k).wait_recv()
         tile(k, first_five)
     s_stage(3)
     spread_halves(2, 18)
-    ring = ((2, 0), (3, 3), (3, 1), (1, 3), (1, 1), (2, 3), (2, 1))
-    tiles(6, 5, ring)
+    for k in (2, 6):
+        tile(k, ring)
     for k in (3, 5):
         handed(k).wait_recv()
         tile(k, first_five)
+    tiles(7, 3, ring[5:])
     s_wait(0, 4, 0)
     s_wait(1, 4, 1)
     go(hand(4))
     tile(3, ring)
     tile(5, ring)
-    handed(4).wait_recv()
-    tile(4, first_five + ring)
     for i in (0, 3, 1, 2):
         t_wait_halves(i, 2)
-    tiles(0, 8, ((0, 2), (1, 2), (2, 2), (3, 2)))
+    for k in (3, 5, 2, 6, 1, 7, 0):
+        tile(k, last)
+    handed(4).wait_recv()
+    tile(4, first_five + ring + last)
 
     def row_again():
         rsum[...] = jnp.zeros((8, 2048), F32)

time: 95.5 us -> 94.5 us (0.990)
  Pallas kernels: 94.8 us -> 93.7 us
    pallas_call x1, Pallas kernels: 92.7 us -> 91.7 us  [body(): pl.pallas_call(kernel, out_shape=(jax.ShapeDtypeStruct((D, 128), BF16), j...]
where the time goes in v5:
time: 94.5 us; the launch traced here: 94.3 us
  Pallas kernels  93.7 us (99%)
    pallas_call x1, Pallas kernels, body(): pl.pallas_call(kernel, out_shape=(jax.ShapeDtypeStruct((D, 128), BF16), j...  91.7 us
    pallas_call x1, Pallas kernels, body(): pl.pallas_call(store, out_shape=tuple((jax.ShapeDtypeStruct(r.shape, r.dt...  2.02 us

profile of v5, /device:TPU:1, one launch (start us, length us, event | category | flops | bytes accessed | tf_op | source)
XLA Modules:
  0.0 94.3 jit_solution(471123063616212527)
XLA Ops:
  0.6 91.7 %shard_map.65 = (bf16[300,128]{1,0:T(8,128)(2,1)}, f32[300,128]{1,0:T(8,128)}, f32[300,300]{1,0:T(8,128)}, f32[128]{0:T(128)}, f32[120]{0:T(128)}) custom-call(bf16[300,128]{1,0:T(8,128)(2,1)} %bitcast.4, bf16[300,120]{1,0:T(8,128)(2,1)} %bitcast.5), custom_call_target="tpu_custom_call" | custom-call | tf_op jit(solution)/shard_map/pallas_call | solution.py:545
  92.3 2.0 %shard_map.66 = (bf16[300,128]{1,0:T(8,128)(2,1)}, f32[300,128]{1,0:T(8,128)}, f32[300,300]{1,0:T(8,128)}, f32[128]{0:T(128)}, f32[120]{0:T(128)}) custom-call(bf16[300,128]{1,0:T(8,128)(2,1)} %get-tuple-element.15.refs_0_, f32[300,128]{1,0:T(8,128)} %get-tuple-element.16.refs_1_, f32[300,300]{1,0:T(8,128)} %get-tuple-element.17.refs_2_, ...), custom_call_target="tpu_custom_call" | custom-call | tf_op jit(solution)/shard_map/pallas_call | solution.py:598
